TPU v7x, 32 devices: a whole 2x2x4 slice. The times are simulated.
32 devices in a mesh: tm: 8 (over y, x, core), space: 4 (over z).
Axes of the slice: x: 2, y: 2, z: 4, core: 2. Of those that a mesh axis runs over, the one named last changes fastest.
Arguments:
- initial_state: float32 [1024, 1024], P('space'), may hold values from -6 to 6
- guess_coarse: float32 [8, 1024, 1024], P('tm', 'space'), may hold values from -6 to 6
- force_fine: float32 [8, 1024, 1024], P('tm', 'space'), may hold values from -6 to 6
- force_coarse: float32 [8, 1024, 1024], P('tm', 'space'), may hold values from -6 to 6
- eigen_basis: float32 [1024, 1024], replicated, may hold values from -1 to 1, as said below
- eigen_rates: float32 [1024], replicated, may hold values from 0.02 to 4
- carried_correction: float32 [1024, 1024], replicated, may hold values from -6 to 6
Outputs:
- fine_states: float32 [8, 1024, 1024], P('tm', 'space')
- coarse_states: float32 [8, 1024, 1024], P('tm', 'space')
Inputs may be any that keep to these rules, and one draw needn't show every extreme that they name: `eigen_basis`: an orthogonal matrix: its transpose is its inverse up to float32 rounding.
All inputs are finite; a program needn't handle non-finite values.
Results may differ from a plain program's by a relative error of at most 0.00013.
Values sent between devices are 32-bit elements; how exact they have to be, the bound alone decides.
A program may use at most 128 MiB of HBM per device.

v0:
```python
import functools
import jax
import jax.numpy as jnp
from jax import lax
from jax.experimental import pallas as pl
from jax.experimental.pallas import tpu as pltpu
from jax.sharding import PartitionSpec as P


def halves(block):
    high = block.astype(jnp.bfloat16)
    return high, (block - high.astype(jnp.float32)).astype(jnp.bfloat16)


def dot3(left, right):
    dot = functools.partial(jnp.dot, preferred_element_type=jnp.float32)
    return dot(left[0], right[0]) + dot(left[0], right[1]) + dot(left[1], right[0])


def stages_kernel(
    plan, forced, raw, basis, basis_t, spare, decay, start, sources, fixed, outs, split, split_tall, field, coeffs, sent, held, doubled, send_sem, recv_sem
):
    count = lax.axis_size("space")
    me = lax.axis_index("space")
    rows = held.shape[2]
    barrier = pltpu.get_barrier_semaphore()

    @pl.loop(0, count)
    def _(d):
        @pl.when(d != me)
        def _():
            pl.semaphore_signal(barrier, inc=1, device_id={"space": d}, device_id_type=pl.DeviceIdType.MESH)

    pl.semaphore_wait(barrier, count - 1)

    def span(d):
        return pl.ds(pl.multiple_of(d * rows, rows), rows)

    def peer(k):
        return jnp.where(me < count // 2, count - 1 - k, k)

    def copy(stage, d):
        return pltpu.make_async_remote_copy(
            src_ref=sent.at[stage, d],
            dst_ref=held.at[stage, me],
            send_sem=send_sem.at[stage, d],
            recv_sem=recv_sem.at[stage, me],
            device_id={"space": d},
            device_id_type=pl.DeviceIdType.MESH,
        )

    def arrival(stage, s):
        return pltpu.make_async_remote_copy(
            src_ref=sent.at[stage, s],
            dst_ref=held.at[stage, s],
            send_sem=send_sem.at[stage, s],
            recv_sem=recv_sem.at[stage, s],
            device_id={"space": s},
            device_id_type=pl.DeviceIdType.MESH,
        )

    def exchange(stage, block_for, use, between=None):
        @pl.loop(0, count)
        def _(k):
            d = peer(k)
            block = block_for(d)

            @pl.when(d != me)
            def _():
                sent[stage, d] = block
                copy(stage, d).start()

            @pl.when(d == me)
            def _():
                held[stage, me] = block

        if between is not None:
            between()
        use(me, True)

        @pl.loop(0, count)
        def _(k):
            s = peer(k)

            @pl.when(s != me)
            def _():
                arrival(stage, s).wait_recv()
                use(s, False)

    def split_basis():
        @pl.loop(0, count)
        def _(r):
            high, low = halves(raw[span(r), :])
            basis[0, span(r), :] = high
            basis[1, span(r), :] = low

    def turn_basis():
        @pl.loop(0, count)
        def _(r):
            @pl.loop(0, count)
            def _(c):
                high, low = halves(raw[span(c), span(r)].T)
                basis_t[0, span(r), span(c)] = high
                basis_t[1, span(r), span(c)] = low

    def forward(stage):
        high, low = halves(field[...])
        split[0] = high
        split[1] = low

        def block_for(d):
            return dot3((split[0], split[1]), (basis[0, :, span(d)], basis[1, :, span(d)]))

        def use(s, first):
            part = halves(held[stage, s])

            @pl.loop(0, count)
            def _(r):
                term = dot3((basis_t[0, span(r), span(s)], basis_t[1, span(r), span(s)]), part)
                coeffs[span(r), :] = term if first else coeffs[span(r), :] + term

        exchange(stage, block_for, use, turn_basis if raw is not None and stage == 0 else None)

    def inverse(stage):
        high, low = halves(coeffs[...])
        split_tall[0] = high
        split_tall[1] = low

        def block_for(d):
            block = dot3((basis[0, span(d), :], basis[1, span(d), :]), (split_tall[0], split_tall[1]))
            if spare is not None and stage == len(plan) - 1:
                doubled[0, span(d), :], doubled[1, span(d), :] = halves(block)
            return block

        def keep_spare():
            @pl.loop(0, count)
            def _(r):
                back = dot3((basis_t[0, span(r), :], basis_t[1, span(r), :]), (doubled[0], doubled[1]))
                spare[span(r), :] = back - coeffs[span(r), :]

        def use(s, first):
            part = halves(held[stage, s])

            @pl.loop(0, count)
            def _(r):
                term = dot3(part, (basis_t[0, span(s), span(r)], basis_t[1, span(s), span(r)]))
                field[:, span(r)] = term if first else field[:, span(r)] + term

        exchange(stage, block_for, use, keep_spare if spare is not None and stage == len(plan) - 1 else None)

    def react(source):
        value = field[...]
        field[...] = value + 0.5 * jnp.tanh(value) + source[...]

    sources = list(sources)
    outs = list(outs)
    if raw is not None:
        split_basis()
    if plan[0] == "E":
        field[...] = start[...]
        react(sources.pop(0))
    else:
        coeffs[...] = start[...]
    for stage, kind in enumerate(plan):
        final = stage == len(plan) - 1
        if kind == "E":
            forward(stage)
            coeffs[...] = coeffs[...] * decay[...]
            if stage in forced:
                outs.pop(0)[...] = coeffs[...]
        else:
            inverse(stage)
            if stage in forced:
                outs.pop(0)[...] = field[...]
            if not final:
                if fixed is not None:
                    @pl.when(lax.axis_index("tm") == lax.axis_size("tm") - 1)
                    def _():
                        field[...] = fixed[...]
                react(sources.pop(0))

    for stage in range(len(plan)):
        @pl.loop(0, count)
        def _(d):
            @pl.when(d != me)
            def _():
                copy(stage, d).wait_send()


def stages(plan, forced, number, basis, decay, start, sources, fixed=None):
    grid, rows = decay.shape
    count = grid // rows
    wide, tall = (rows, grid), (grid, rows)
    extra = 0 if fixed is None else 1
    first = not isinstance(basis, tuple)
    given = [basis] if first else list(basis)
    shapes = [jax.ShapeDtypeStruct(tall if plan[s] == "E" else wide, jnp.float32) for s in forced]
    if first:
        shapes += [jax.ShapeDtypeStruct((2, grid, grid), jnp.bfloat16)] * 2 + [jax.ShapeDtypeStruct(tall, jnp.float32)]

    def kernel(*refs):
        refs = list(refs)
        basis_refs = refs[: len(given)]
        del refs[: len(given)]
        decay_ref, start_ref = refs[:2]
        del refs[:2]
        source_refs = refs[: len(sources)]
        del refs[: len(sources)]
        fixed_ref = refs.pop(0) if extra else None
        out_refs = refs[: len(shapes)]
        raw, spare = None, None
        if first:
            raw = basis_refs[0]
            basis_refs, spare = out_refs[-3:-1], out_refs[-1]
        stages_kernel(
            plan, forced, raw, *basis_refs, spare, decay_ref, start_ref, source_refs, fixed_ref, out_refs, *refs[len(shapes):]
        )

    operands = [*given, decay, start, *sources] + ([fixed] if extra else [])
    steps = len(plan)
    vmem = pl.BlockSpec(memory_space=pltpu.VMEM)
    return pl.pallas_call(
        kernel,
        out_shape=shapes,
        in_specs=[vmem] * len(operands),
        out_specs=[vmem] * len(shapes),
        scratch_shapes=[
            pltpu.VMEM((2, *wide), jnp.bfloat16),
            pltpu.VMEM((2, *tall), jnp.bfloat16),
            pltpu.VMEM(wide, jnp.float32),
            pltpu.VMEM(tall, jnp.float32),
            pltpu.VMEM((steps, count, rows, rows), jnp.float32),
            pltpu.VMEM((steps, count, rows, rows), jnp.float32),
            pltpu.VMEM((2, *tall) if first else (2, 16, 128), jnp.bfloat16),
            pltpu.SemaphoreType.DMA((steps, count)),
            pltpu.SemaphoreType.DMA((steps, count)),
        ],
        compiler_params=pltpu.CompilerParams(
            collective_id=number, has_side_effects=True, vmem_limit_bytes=48 * 1024 * 1024
        ),
        cost_estimate=pl.CostEstimate(
            flops=steps * 40_000_000_000, bytes_accessed=8 * grid * grid, transcendentals=0
        ),
        name="stages_%d" % number,
    )(*operands)


def decay_block(eigen_rates, own_rates, factor):
    return 1.0 / (1.0 + factor * (eigen_rates[:, None] + own_rates[None, :]))


def shift(block, distance):
    count = lax.axis_size("tm")
    return lax.ppermute(block, "tm", [(i, (i + distance) % count) for i in range(count)])


def swap(block):
    count = lax.axis_size("tm")
    return lax.ppermute(block, "tm", [(i, i ^ 1) for i in range(count)])


def coarse_solve(terms, start, decay):
    count = lax.axis_size("tm")
    pairs = count // 2
    place = lax.axis_index("tm")
    pair, odd = place // 2, place % 2
    half = terms.shape[0] // 2

    def mine(block, which):
        return lax.dynamic_slice_in_dim(block, which * half, half, 0)

    other = swap(mine(terms, 1 - odd))
    own = mine(terms, odd)
    first = jnp.where(odd == 0, own, other)
    second = jnp.where(odd == 0, other, own)
    decay = mine(decay, odd)
    carried = mine(start, odd)
    is_last = pair == pairs - 1
    sums = second + decay * jnp.where(is_last, carried, first)
    squared = decay * decay
    before = jnp.where(is_last, sums, 0.0)
    arrived = {}
    for s in range(1, pairs):
        route = []
        for k in range(pairs):
            if s <= k + 1:
                source = (k - s) % pairs
                route += [(2 * source + c, 2 * k + c) for c in range(2)]
        arrived[s] = lax.ppermute(sums, "tm", route)
    for s in range(pairs - 1, 0, -1):
        before = squared * before + arrived[s]
    even_state = before
    odd_state = first + decay * even_state
    given = jnp.where(odd == 0, odd_state, even_state)
    kept = jnp.where(odd == 0, even_state, odd_state)
    got = swap(given)
    return jnp.where(
        odd == 0,
        jnp.concatenate([kept, got], 0),
        jnp.concatenate([got, kept], 0),
    )


def on_device(
    initial_state,
    guess_coarse,
    force_fine,
    force_coarse,
    eigen_basis,
    eigen_rates,
    carried_correction,
):
    row_count = initial_state.shape[0]
    offset = lax.axis_index("space") * row_count
    own_rates = lax.dynamic_slice_in_dim(eigen_rates, offset, row_count, 0)
    fine_decay = decay_block(eigen_rates, own_rates, 1.0)
    coarse_decay = decay_block(eigen_rates, own_rates, 2.0)
    carried = lax.dynamic_slice_in_dim(carried_correction, offset, row_count, 1)
    place = lax.axis_index("tm")
    at_start = place == 0
    at_end = place == lax.axis_size("tm") - 1
    fine_here, coarse_here = force_fine[0], force_coarse[0]
    fine_next, coarse_next = shift(fine_here, -1), shift(coarse_here, -1)
    run = functools.partial(stages, decay=fine_decay)

    entering = jnp.where(at_start, initial_state, shift(guess_coarse[0], 1))
    relaxed, relaxed_coarse, basis, basis_t, gathered = run(
        "EIEI", (2, 3), 1, basis=eigen_basis, start=entering, sources=[fine_here, coarse_here]
    )
    run = functools.partial(run, basis=(basis, basis_t))
    from_here = jnp.where(at_end, initial_state, relaxed_coarse)
    (target,) = run("EIE", (2,), 2, start=from_here, sources=[fine_next, coarse_next])
    terms = target - jnp.where(at_end, 0.0, coarse_decay * (relaxed + gathered))
    states = coarse_solve(terms, carried, coarse_decay) - gathered
    coarse_new, fine_new = run("IEI", (0, 2), 3, start=states, sources=[fine_next], fixed=initial_state)
    return (shift(fine_new, 1)[None], coarse_new[None])


def solution(mesh):
    placed = (
        P("space", None),
        P("tm", "space", None),
        P("tm", "space", None),
        P("tm", "space", None),
        P(),
        P(),
        P(),
    )
    return jax.shard_map(
        on_device,
        mesh=mesh,
        in_specs=placed,
        out_specs=(P("tm", "space", None), P("tm", "space", None)),
        check_vma=False,
    )
```

profile of v0, /device:TPU:12, one launch (start us, length us, event | category | flops | bytes accessed | tf_op | source)
XLA Modules:
  0.0 349.7 jit_solution(15335126377501092974)
XLA Ops:
  0.6 0.1 collective-permute-start
  0.7 2.6 collective-permute-start.1
  3.3 0.0 collective-permute-start.2
  3.4 0.8 dynamic_slice.16
  4.1 0.0 copy-start.3
  4.1 0.9 fusion.refs_1_.refs_2_
  5.0 0.0 copy-done.3
  5.0 21.4 %collective-permute-done = f32[256,1024]{1,0:T(8,128)S(1)} collective-permute-done((f32[256,1024]{1,0:T(8,128)}, f32[256,1024]{1,0:T(8,128)S(1)}, u32[]{:S(2)}, u32[]{:S(2)}) %collective-permute-start) | collective-permute-done | bytes 1048608 | tf_op jit(solution)/shard_map/ppermute | solution.py:254
  26.4 0.1 broadcast_select_fusion.1.refs_2_
  26.6 0.0 copy-start.1
  26.6 107.1 %stages_1.1 = (f32[1024,256]{1,0:T(8,128)S(1)}, f32[256,1024]{1,0:T(8,128)S(1)}, bf16[2,1024,1024]{2,1,0:T(8,128)(2,1)}, bf16[2,1024,1024]{2,1,0:T(8,128)(2,1)}, f32[1024,256]{1,0:T(8,128)S(1)}) custom-call(f32[1024,1024]{1,0:T(8,128)} %refs_0_.1, f32[1024,256]{1,0:T(8,128)S(1)} %fusion.refs_1_.refs_2_, f32[256,1024]{1,0:T(8,128)S(1)} %broadcast_select_fusion.1.refs_2_, ...), custom_call_target="tpu_custom_call" | custom-call | flops 160000000000 | bytes 8388608 | tf_op jit(solution)/shard_map/stages_1/pallas_call | solution.py:222
  133.7 0.0 copy-done.1
  133.7 0.2 broadcast_select_fusion.refs_3_
  133.9 0.0 collective-permute-done.1.refs_4_
  133.9 0.0 collective-permute-done.2.refs_5_
  133.9 0.0 copy-start.2
  133.9 0.0 copy-start.4
  133.9 78.0 %stages_2.1 = f32[1024,256]{1,0:T(8,128)S(1)} custom-call(bf16[2,1024,1024]{2,1,0:T(8,128)(2,1)} %get-tuple-element.9.refs_0_, bf16[2,1024,1024]{2,1,0:T(8,128)(2,1)} %get-tuple-element.10.refs_1_, f32[1024,256]{1,0:T(8,128)S(1)} %fusion.refs_1_.refs_2_, f32[256,1024]{1,0:T(8,128)S(1)} %broadcast_select_fusion.refs_3_, ...), custom_call_target="tpu_custom_call" | custom-call | flops 120000004096 | bytes 8388608 | tf_op jit(solution)/shard_map/stages_2/pallas_call | solution.py:222
  212.0 0.0 copy-done.2
  212.0 0.0 copy-done.4
  212.0 1.3 select_subtract_fusion
  213.3 0.8 constant_dynamic-slice_fusion
  214.1 0.0 collective-permute-start.3
  214.1 0.0 copy-start
  214.1 2.2 collective-permute-done.3
  216.4 1.7 multiply_add_fusion.2
  218.0 0.4 collective-permute-start.6
  218.4 1.3 collective-permute-start.5
  219.7 1.3 collective-permute-start.4
  221.0 12.1 %collective-permute-done.6 = f32[512,256]{1,0:T(8,128)S(1)} collective-permute-done((f32[512,256]{1,0:T(8,128)S(1)}, f32[512,256]{1,0:T(8,128)S(1)}, u32[]{:S(2)}, u32[]{:S(2)}) %collective-permute-start.6) | collective-permute-done | bytes 524320 | tf_op jit(solution)/shard_map/ppermute | solution.py:289
  233.1 11.1 %collective-permute-done.5 = f32[512,256]{1,0:T(8,128)S(1)} collective-permute-done((f32[512,256]{1,0:T(8,128)S(1)}, f32[512,256]{1,0:T(8,128)S(1)}, u32[]{:S(2)}, u32[]{:S(2)}) %collective-permute-start.5) | collective-permute-done | bytes 524320 | tf_op jit(solution)/shard_map/ppermute | solution.py:289
  244.2 0.0 collective-permute-done.4
  244.2 1.4 broadcast_select_fusion.3
  245.6 0.0 copy-done
  245.6 0.2 broadcast_select_fusion.2
  245.7 1.3 collective-permute-start.7
  247.0 1.5 collective-permute-done.7
  248.6 0.2 fusion.3.refs_3_
  248.7 83.9 %stages_3.1 = (f32[256,1024]{1,0:T(8,128)S(1)}, f32[256,1024]{1,0:T(8,128)S(1)}) custom-call(bf16[2,1024,1024]{2,1,0:T(8,128)(2,1)} %get-tuple-element.9.refs_0_, bf16[2,1024,1024]{2,1,0:T(8,128)(2,1)} %get-tuple-element.10.refs_1_, f32[1024,256]{1,0:T(8,128)S(1)} %fusion.refs_1_.refs_2_, f32[1024,256]{1,0:T(8,128)S(1)} %fusion.3.refs_3_, ...), custom_call_target="tpu_custom_call" | custom-call | flops 120000004096 | bytes 8388608 | tf_op jit(solution)/shard_map/stages_3/pallas_call | solution.py:222
  332.6 0.1 collective-permute-start.8
  332.7 15.1 %collective-permute-done.8 = f32[256,1024]{1,0:T(8,128)S(1)} collective-permute-done((f32[256,1024]{1,0:T(8,128)S(1)}, f32[256,1024]{1,0:T(8,128)S(1)}, u32[]{:S(2)}, u32[]{:S(2)}) %collective-permute-start.8) | collective-permute-done | bytes 1048608 | tf_op jit(solution)/shard_map/ppermute | solution.py:254
  347.8 1.0 copy.11
  348.8 1.0 copy.12
Async XLA Ops:
  0.6 25.8 %collective-permute-start = (f32[256,1024]{1,0:T(8,128)}, f32[256,1024]{1,0:T(8,128)S(1)}, u32[]{:S(2)}, u32[]{:S(2)}) collective-permute-start(f32[256,1024]{1,0:T(8,128)} %bitcast.7), channel_id=1, source_target_pairs={{0,4},{4,8},{8,12},{12,16},{16,20},{20,24},{24,28},{28,0},{1,5},{5... | collective-permute-start | bytes 3145736 | tf_op jit(solution)/shard_map/ppermute | solution.py:254
  0.7 133.2 %collective-permute-start.1 = (f32[256,1024]{1,0:T(8,128)}, f32[256,1024]{1,0:T(8,128)}, u32[]{:S(2)}, u32[]{:S(2)}) collective-permute-start(f32[256,1024]{1,0:T(8,128)} %bitcast.8), channel_id=1, source_target_pairs={{0,28},{4,0},{8,4},{12,8},{16,12},{20,16},{24,20},{28,24},{1,29},{... | collective-permute-start | bytes 3145736 | tf_op jit(solution)/shard_map/ppermute | solution.py:254
  3.3 130.6 %collective-permute-start.2 = (f32[256,1024]{1,0:T(8,128)}, f32[256,1024]{1,0:T(8,128)}, u32[]{:S(2)}, u32[]{:S(2)}) collective-permute-start(f32[256,1024]{1,0:T(8,128)} %bitcast.10), channel_id=1, source_target_pairs={{0,28},{4,0},{8,4},{12,8},{16,12},{20,16},{24,20},{28,24},{1,29},{... | collective-permute-start | bytes 3145736 | tf_op jit(solution)/shard_map/ppermute | solution.py:254
  4.1 0.9 copy-start.3
  26.6 107.1 %copy-start.1 = (f32[256,1024]{1,0:T(8,128)S(1)}, f32[256,1024]{1,0:T(8,128)}, u32[]{:S(2)}) copy-start(f32[256,1024]{1,0:T(8,128)} %refs_5_.1) | copy-start | bytes 3145732
  133.9 78.1 %copy-start.2 = (f32[1024]{0:T(1024)S(1)}, f32[1024]{0:T(1024)}, u32[]{:S(2)}) copy-start(f32[1024]{0:T(1024)} %param.12) | copy-start | bytes 12292
  133.9 78.1 %copy-start.4 = (f32[256]{0:T(256)S(1)}, f32[256]{0:T(256)}, u32[]{:S(2)}) copy-start(f32[256]{0:T(256)} %copy-done.3) | copy-start | bytes 3076
  214.1 2.3 collective-permute-start.3
  214.1 31.4 %copy-start = (f32[1024,256]{1,0:T(8,128)S(1)}, f32[1024,256]{1,0:T(8,128)}, u32[]{:S(2)}) copy-start(f32[1024,256]{1,0:T(8,128)} %get-tuple-element.19) | copy-start | bytes 3145732
  218.0 15.0 %collective-permute-start.6 = (f32[512,256]{1,0:T(8,128)S(1)}, f32[512,256]{1,0:T(8,128)S(1)}, u32[]{:S(2)}, u32[]{:S(2)}) collective-permute-start(f32[512,256]{1,0:T(8,128)S(1)} %multiply_add_fusion.2), channel_id=1, source_target_pairs={{24,0},{28,4},{0,8},{4,12},{8,16},{12,20},{16,24},{20,28},{25,1},{... | collective-permute-start | bytes 1572872 | tf_op jit(solution)/shard_map/ppermute | solution.py:289
  218.4 25.8 %collective-permute-start.5 = (f32[512,256]{1,0:T(8,128)S(1)}, f32[512,256]{1,0:T(8,128)S(1)}, u32[]{:S(2)}, u32[]{:S(2)}) collective-permute-start(f32[512,256]{1,0:T(8,128)S(1)} %multiply_add_fusion.2), channel_id=1, source_target_pairs={{24,8},{28,12},{0,16},{4,20},{8,24},{12,28},{25,9},{29,13},{1,17},... | collective-permute-start | bytes 1572872 | tf_op jit(solution)/shard_map/ppermute | solution.py:289
  219.7 24.5 %collective-permute-start.4 = (f32[512,256]{1,0:T(8,128)S(1)}, f32[512,256]{1,0:T(8,128)S(1)}, u32[]{:S(2)}, u32[]{:S(2)}) collective-permute-start(f32[512,256]{1,0:T(8,128)S(1)} %multiply_add_fusion.2), channel_id=1, source_target_pairs={{24,16},{28,20},{0,24},{4,28},{25,17},{29,21},{1,25},{5,29},{26,18... | collective-permute-start | bytes 1572872 | tf_op jit(solution)/shard_map/ppermute | solution.py:289
  245.7 2.8 collective-permute-start.7
  332.6 15.2 %collective-permute-start.8 = (f32[256,1024]{1,0:T(8,128)S(1)}, f32[256,1024]{1,0:T(8,128)S(1)}, u32[]{:S(2)}, u32[]{:S(2)}) collective-permute-start(f32[256,1024]{1,0:T(8,128)S(1)} %get-tuple-element.14), channel_id=1, source_target_pairs={{0,4},{4,8},{8,12},{12,16},{16,20},{20,24},{24,28},{28,0},{1,5},{5... | collective-permute-start | bytes 3145736 | tf_op jit(solution)/shard_map/ppermute | solution.py:254
where the time goes:
time: 350 us
  Pallas kernels  269 us (77%)
  waiting for transfers between devices  63.5 us (18%)
  starting transfers between devices  7.02 us (2%)
  other arithmetic  5.89 us (2%)
  local copies, waits for them, and re-layouts  3.55 us (1%)
    pallas_call x3, Pallas kernels, stages(): pl.pallas_call(kernel, out_shape=shapes, in_specs=[vmem] * len(operands),...  269 us
    ppermute x4, waiting for transfers between devices, shift(): lax.ppermute(block, 'tm', [(i, (i + distance) % count) for i in range(cou...  36.5 us
    ppermute x3, waiting for transfers between devices, coarse_solve(): arrived[s] = lax.ppermute(sums, 'tm', route)  23.2 us
  transfers between devices with their start and end apart: 9, of which 6 were waited for; matrix products, arithmetic and copies ran while one was open for 1% of the time, Pallas kernels for 31%

commit v1 on v0

--- a/solution.py
+++ b/solution.py
@@ -6,6 +6,8 @@
 from jax.experimental.pallas import tpu as pltpu
 from jax.sharding import PartitionSpec as P
 
+MESH = pl.DeviceIdType.MESH
+
 
 def halves(block):
     high = block.astype(jnp.bfloat16)
@@ -15,6 +17,360 @@
 def dot3(left, right):
     dot = functools.partial(jnp.dot, preferred_element_type=jnp.float32)
     return dot(left[0], right[0]) + dot(left[0], right[1]) + dot(left[1], right[0])
+
+
+def reacted(value):
+    return value + 0.5 * jnp.tanh(value)
+
+
+def chain_kernel(
+    raw, rates_tall, rates_wide, guess, initial, fine, coarse, basis, basis_t, terms,
+    before, entry, slots, field, coeffs, kept, wide, tall, part, sent, held, decay, coarse_decay, leaving, landed,
+    home_send, shift_recv, slot_recv, ex_send, ex_recv, term_send, term_recv,
+):
+    groups, count = lax.axis_size("tm"), lax.axis_size("space")
+    t, s = lax.axis_index("tm"), lax.axis_index("space")
+    grid = raw.shape[0]
+    rows = fine.shape[0]
+    half = grid // 2
+    piece = half // 2
+    per_half = count // 2
+    low_seat = per_half - 1
+    last = groups - 1
+
+    def at(start, size):
+        return pl.ds(pl.multiple_of(start, size), size)
+
+    def seat(chain):
+        return low_seat + chain % 2
+
+    def core(chain, which):
+        return 2 * (chain // 2) + which
+
+    which = s // per_half
+    place = at((s % per_half) * rows, rows)
+    mine, past = t, (t + groups - 1) % groups
+    mine_at = (core(mine, which), seat(mine))
+    past_at = (core(past, which), seat(past))
+    to_self = (mine_at[0] == t) & (mine_at[1] == s)
+
+    def remote(src, dst, send, recv, where):
+        return pltpu.make_async_remote_copy(
+            src_ref=src, dst_ref=dst, send_sem=send, recv_sem=recv,
+            device_id={"tm": where[0], "space": where[1]}, device_id_type=MESH,
+        )
+
+    def to_mine(src, slot, index):
+        pos = s % per_half
+        dst, recv = slots.at[slot, place], slot_recv.at[slot, pos]
+
+        @pl.when(jnp.logical_not(to_self))
+        def _():
+            remote(src, dst, home_send.at[index], recv, mine_at).start()
+
+        @pl.when(to_self)
+        def _():
+            pltpu.make_async_copy(src, dst, recv).start()
+
+    def to_past(src, slot, index):
+        return remote(src, slots.at[slot, place], home_send.at[index], slot_recv.at[slot, s % per_half], past_at)
+
+    def pass_on():
+        return remote(guess, before, home_send.at[4], shift_recv.at[0], ((t + 1) % groups, s))
+
+    @pl.when(t != last)
+    def _():
+        pass_on().start()
+
+    to_mine(coarse, 1, 0)
+
+    @pl.loop(0, count)
+    def _(r):
+        high, low = halves(raw[at(r * rows, rows), :])
+        basis[0, at(r * rows, rows), :] = high
+        basis[1, at(r * rows, rows), :] = low
+
+    @pl.when(t != 0)
+    def _():
+        remote(guess, before, home_send.at[4], shift_recv.at[0], (t, s)).wait_recv()
+        entry[...] = reacted(before[...]) + fine[...]
+
+    @pl.when(t == 0)
+    def _():
+        entry[...] = reacted(initial[...]) + fine[...]
+
+    to_mine(entry, 0, 1)
+
+    @pl.when(t == 0)
+    def _():
+        to_past(entry, 2, 2).start()
+
+    @pl.when(t != 0)
+    def _():
+        to_past(fine, 2, 2).start()
+
+    to_past(coarse, 3, 3).start()
+
+    @pl.loop(0, grid // piece)
+    def _(r):
+        @pl.loop(0, grid // piece)
+        def _(c):
+            high, low = halves(raw[at(c * piece, piece), at(r * piece, piece)].T)
+            basis_t[0, at(r * piece, piece), at(c * piece, piece)] = high
+            basis_t[1, at(r * piece, piece), at(c * piece, piece)] = low
+
+    side = t % 2
+    group = 2 * (t // 2) + (s - low_seat)
+    partner = (2 * (t // 2) + 1 - side, s)
+    own, other = at(side * half, half), at((1 - side) * half, half)
+
+    def wait_slot(slot, position):
+        source = side * per_half + position
+        dst, recv = slots.at[slot, at(position * rows, rows)], slot_recv.at[slot, position]
+        local = (group == t) & (source == s) if slot < 2 else None
+
+        def arrive():
+            remote(fine, dst, home_send.at[0], recv, (t, s)).wait_recv()
+
+        if local is None:
+            arrive()
+        else:
+            pl.when(jnp.logical_not(local))(arrive)
+
+            @pl.when(local)
+            def _():
+                pltpu.make_async_copy(fine, dst, recv).wait()
+
+    def exchange(stage, m):
+        block = at(m * piece, piece)
+        return remote(sent.at[stage % 2, block], held.at[stage % 2, block], ex_send.at[stage, m], ex_recv.at[stage, m], partner)
+
+    def collect(stage):
+        for m in range(2):
+            exchange(stage, m).wait_recv()
+            part[0, m * piece:(m + 1) * piece, :], part[1, m * piece:(m + 1) * piece, :] = halves(
+                held[stage % 2, m * piece:(m + 1) * piece, :]
+            )
+
+    def take(stage, make):
+        if stage >= 2:
+            for m in range(2):
+                exchange(stage - 2, m).wait_send()
+
+        @pl.loop(0, 2)
+        def _(m):
+            sent[stage % 2, at(m * piece, piece)] = make(m, False)
+            exchange(stage, m).start()
+
+        @pl.loop(0, 2)
+        def _(m):
+            block = at(m * piece, piece)
+            part[0, block, :], part[1, block, :] = halves(make(m, True))
+
+    def forward(stage, source, ready, finish):
+        for m in range(per_half):
+            ready(m)
+            high, low = halves(source(at(m * rows, rows)))
+            wide[0, at(m * rows, rows), :] = high
+            wide[1, at(m * rows, rows), :] = low
+
+        def make(m, keep):
+            block, columns = at(m * piece, piece), own if keep else other
+            return dot3((wide[0, block, :], wide[1, block, :]), (basis[0, :, columns], basis[1, :, columns]))
+
+        take(stage, make)
+
+        @pl.loop(0, grid // piece)
+        def _(r):
+            block = at(r * piece, piece)
+            coeffs[block, :] = dot3((basis_t[0, block, own], basis_t[1, block, own]), (part[0], part[1]))
+
+        collect(stage)
+
+        @pl.loop(0, grid // piece)
+        def _(r):
+            block = at(r * piece, piece)
+            term = dot3((basis_t[0, block, other], basis_t[1, block, other]), (part[0], part[1]))
+            finish(r, block, (coeffs[block, :] + term) * decay[block, :])
+
+    def inverse(stage):
+        @pl.loop(0, grid // piece)
+        def _(r):
+            block = at(r * piece, piece)
+            tall[0, block, :], tall[1, block, :] = halves(coeffs[block, :])
+
+        def make(m, keep):
+            block = at((side if keep else 1 - side) * half + m * piece, piece)
+            return dot3((basis[0, block, :], basis[1, block, :]), (tall[0], tall[1]))
+
+        take(stage, make)
+
+        @pl.loop(0, 2)
+        def _(n):
+            columns = at(n * half, half)
+            field[:, columns] = dot3((part[0], part[1]), (basis_t[0, own, columns], basis_t[1, own, columns]))
+
+        collect(stage)
+
+        @pl.loop(0, 2)
+        def _(n):
+            columns = at(n * half, half)
+            field[:, columns] = field[:, columns] + dot3(
+                (part[0], part[1]), (basis_t[0, other, columns], basis_t[1, other, columns])
+            )
+
+    @pl.when((s == low_seat) | (s == low_seat + 1))
+    def _():
+        @pl.loop(0, grid // piece)
+        def _(r):
+            block = at(r * piece, piece)
+            pair = rates_tall[block, :1] + rates_wide[:1, own]
+            decay[block, :] = 1.0 / (1.0 + pair)
+            coarse_decay[block, :] = 1.0 / (1.0 + 2.0 * pair)
+
+        def plain(r, block, value):
+            coeffs[block, :] = value
+
+        def keep(r, block, value):
+            coeffs[block, :] = value
+            kept[block, :] = jnp.where(group == last, 0.0, value * coarse_decay[block, :])
+
+        def leave(r, block, value):
+            value = value - kept[block, :]
+            for q in range(per_half):
+                leaving[q, block, :] = value[:, q * rows:(q + 1) * rows]
+            for q in range(per_half):
+                send_term(r, q)
+
+        def term_place(q):
+            return group, side * per_half + q
+
+        def term_copy(r, q):
+            block = at(r * piece, piece)
+            return remote(leaving.at[q, block], landed.at[block], term_send.at[q, r], term_recv.at[r], term_place(q))
+
+        def term_local(r, q):
+            block = at(r * piece, piece)
+            return pltpu.make_async_copy(leaving.at[q, block], landed.at[block], term_recv.at[r])
+
+        def term_here(q):
+            where = term_place(q)
+            return (where[0] == t) & (where[1] == s)
+
+        def send_term(r, q):
+            here = term_here(q)
+
+            @pl.when(here)
+            def _():
+                term_local(r, q).start()
+
+            @pl.when(jnp.logical_not(here))
+            def _():
+                term_copy(r, q).start()
+
+        def from_field(slot):
+            def source(block):
+                moved = reacted(field[block, :])
+                if slot == 2:
+                    moved = jnp.where(group == last, 0.0, moved)
+                return moved + slots[slot, block, :]
+            return source
+
+        forward(0, lambda block: slots[0, block, :], lambda m: wait_slot(0, m), plain)
+        inverse(1)
+        forward(2, from_field(1), lambda m: wait_slot(1, m), keep)
+        inverse(3)
+        forward(4, from_field(2), lambda m: wait_slot(2, m), plain)
+        inverse(5)
+        forward(6, from_field(3), lambda m: wait_slot(3, m), leave)
+
+        for stage in (5, 6):
+            for m in range(2):
+                exchange(stage, m).wait_send()
+        for q in range(per_half):
+            @pl.when(jnp.logical_not(term_here(q)))
+            def _():
+                for r in range(grid // piece):
+                    term_copy(r, q).wait_send()
+
+    term_side = s // per_half
+    sender = (core(t, term_side), seat(t))
+    from_self = (sender[0] == t) & (sender[1] == s)
+    for r in range(grid // piece):
+        block = at(r * piece, piece)
+
+        @pl.when(from_self)
+        def _():
+            pltpu.make_async_copy(leaving.at[0, block], landed.at[block], term_recv.at[r]).wait()
+
+        @pl.when(jnp.logical_not(from_self))
+        def _():
+            remote(leaving.at[0, block], landed.at[block], term_send.at[0, r], term_recv.at[r], (t, s)).wait_recv()
+
+        terms[block, :] = landed[block, :]
+
+    @pl.when(jnp.logical_not(to_self))
+    def _():
+        for index, src in ((0, coarse), (1, entry)):
+            remote(src, slots.at[0, place], home_send.at[index], slot_recv.at[0, 0], mine_at).wait_send()
+
+    for index in (2, 3):
+        remote(fine, slots.at[0, place], home_send.at[index], slot_recv.at[0, 0], past_at).wait_send()
+
+    @pl.when(t != last)
+    def _():
+        pass_on().wait_send()
+
+
+def chains(basis, rates, guess, initial, fine, coarse):
+    grid, rows = basis.shape[0], fine.shape[0]
+    half = grid // 2
+    piece, count = half // 2, grid // rows
+    per_half = count // 2
+    steps = 7
+    f32, bf16 = jnp.float32, jnp.bfloat16
+    lanes = 128
+    operands = [basis, jnp.broadcast_to(rates[:, None], (grid, lanes)), rates[None, :], guess, initial, fine, coarse]
+    shapes = [
+        jax.ShapeDtypeStruct((2, grid, grid), bf16),
+        jax.ShapeDtypeStruct((2, grid, grid), bf16),
+        jax.ShapeDtypeStruct((grid, rows), f32),
+    ]
+    vmem = pl.BlockSpec(memory_space=pltpu.VMEM)
+    dma = pltpu.SemaphoreType.DMA
+    return pl.pallas_call(
+        chain_kernel,
+        out_shape=shapes,
+        in_specs=[vmem] * len(operands),
+        out_specs=[vmem] * len(shapes),
+        scratch_shapes=[
+            pltpu.VMEM((rows, grid), f32),
+            pltpu.VMEM((rows, grid), f32),
+            pltpu.VMEM((4, half, grid), f32),
+            pltpu.VMEM((half, grid), f32),
+            pltpu.VMEM((grid, half), f32),
+            pltpu.VMEM((grid, half), f32),
+            pltpu.VMEM((2, half, grid), bf16),
+            pltpu.VMEM((2, grid, half), bf16),
+            pltpu.VMEM((2, half, half), bf16),
+            pltpu.VMEM((2, half, half), f32),
+            pltpu.VMEM((2, half, half), f32),
+            pltpu.VMEM((grid, half), f32),
+            pltpu.VMEM((grid, half), f32),
+            pltpu.VMEM((per_half, grid, rows), f32),
+            pltpu.VMEM((grid, rows), f32),
+            dma((5,)),
+            dma((1,)),
+            dma((4, per_half)),
+            dma((steps, 2)),
+            dma((steps, 2)),
+            dma((per_half, grid // piece)),
+            dma((grid // piece,)),
+        ],
+        compiler_params=pltpu.CompilerParams(has_side_effects=True, vmem_limit_bytes=62 * 1024 * 1024),
+        cost_estimate=pl.CostEstimate(flops=150_000_000_000, bytes_accessed=16 * grid * grid, transcendentals=0),
+        name="chains",
+    )(*operands)
 
 
 def stages_kernel(
@@ -317,22 +673,14 @@
     coarse_decay = decay_block(eigen_rates, own_rates, 2.0)
     carried = lax.dynamic_slice_in_dim(carried_correction, offset, row_count, 1)
     place = lax.axis_index("tm")
-    at_start = place == 0
-    at_end = place == lax.axis_size("tm") - 1
-    fine_here, coarse_here = force_fine[0], force_coarse[0]
-    fine_next, coarse_next = shift(fine_here, -1), shift(coarse_here, -1)
-    run = functools.partial(stages, decay=fine_decay)
-
-    entering = jnp.where(at_start, initial_state, shift(guess_coarse[0], 1))
-    relaxed, relaxed_coarse, basis, basis_t, gathered = run(
-        "EIEI", (2, 3), 1, basis=eigen_basis, start=entering, sources=[fine_here, coarse_here]
+    basis, basis_t, terms = chains(
+        eigen_basis, eigen_rates, guess_coarse[0], initial_state, force_fine[0], force_coarse[0]
     )
-    run = functools.partial(run, basis=(basis, basis_t))
-    from_here = jnp.where(at_end, initial_state, relaxed_coarse)
-    (target,) = run("EIE", (2,), 2, start=from_here, sources=[fine_next, coarse_next])
-    terms = target - jnp.where(at_end, 0.0, coarse_decay * (relaxed + gathered))
-    states = coarse_solve(terms, carried, coarse_decay) - gathered
-    coarse_new, fine_new = run("IEI", (0, 2), 3, start=states, sources=[fine_next], fixed=initial_state)
+    fine_next = shift(force_fine[0], -1)
+    states = coarse_solve(terms, carried, coarse_decay)
+    coarse_new, fine_new = stages(
+        "IEI", (0, 2), 3, basis=(basis, basis_t), decay=fine_decay, start=states, sources=[fine_next], fixed=initial_state
+    )
     return (shift(fine_new, 1)[None], coarse_new[None])
 
 

time: 350 us -> 355 us (1.014); the launches traced: 350 us -> 350 us
  starting transfers between devices: 7.02 us -> 41.7 us
  waiting for transfers between devices: 63.5 us -> 43.3 us
  Pallas kernels: 269 us -> 257 us
  other arithmetic: 5.89 us -> 2.1 us
    pallas_call x3 -> x1, Pallas kernels: 269 us -> 82.8 us  [stages(): pl.pallas_call(kernel, out_shape=shapes, in_specs=[vmem] * len(operands),...]
    pallas_call x0 -> x1, Pallas kernels: none -> 174 us  [chains(): pl.pallas_call(chain_kernel, out_shape=shapes, in_specs=[vmem] * len(oper...]
    ppermute x2, starting transfers between devices: 1.29 us -> 30.1 us  [swap(): return lax.ppermute(block, 'tm', [(i, i ^ 1) for i in range(count)])]
    ppermute x4 -> x2, waiting for transfers between devices: 36.5 us -> 20.3 us  [shift(): lax.ppermute(block, 'tm', [(i, (i + distance) % count) for i in range(cou...]
    ppermute x4 -> x2, starting transfers between devices: 2.79 us -> 7.12 us  [shift(): lax.ppermute(block, 'tm', [(i, (i + distance) % count) for i in range(cou...]
  transfers between devices with their start and end apart: 9 -> 7, of which waited for: 6 -> 6; matrix products, arithmetic and copies ran while one was open for 1% -> 0% of each run, Pallas kernels for 31% -> 0%
where the time goes in v1:
time: 355 us; the launch traced here: 350 us
  Pallas kernels  257 us (72%)
  waiting for transfers between devices  43.3 us (12%)
  starting transfers between devices  41.7 us (12%)
  local copies, waits for them, and re-layouts  4.94 us (1%)
    pallas_call x1, Pallas kernels, chains(): pl.pallas_call(chain_kernel, out_shape=shapes, in_specs=[vmem] * len(oper...  174 us
    pallas_call x1, Pallas kernels, stages(): pl.pallas_call(kernel, out_shape=shapes, in_specs=[vmem] * len(operands),...  82.8 us
    ppermute x2, starting transfers between devices, swap(): return lax.ppermute(block, 'tm', [(i, i ^ 1) for i in range(count)])  30.1 us
    ppermute x2, waiting for transfers between devices, shift(): lax.ppermute(block, 'tm', [(i, (i + distance) % count) for i in range(cou...  20.3 us
    ppermute x3, waiting for transfers between devices, coarse_solve(): arrived[s] = lax.ppermute(sums, 'tm', route)  19.9 us
    ppermute x2, starting transfers between devices, shift(): lax.ppermute(block, 'tm', [(i, (i + distance) % count) for i in range(cou...  7.12 us
  transfers between devices with their start and end apart: 7, of which 6 were waited for; matrix products, arithmetic and copies ran while one was open for 0% of the time, Pallas kernels for 0%

profile of v1, /device:TPU:12, one launch (start us, length us, event | category | flops | bytes accessed | tf_op | source)
XLA Modules:
  0.0 349.8 jit_solution(15861373746755466984)
XLA Ops:
  0.7 1.7 broadcast_in_dim.12.rates_tall
  2.3 0.0 copy-start.1
  2.3 174.3 %chains.1 = (bf16[2,1024,1024]{2,1,0:T(8,128)(2,1)}, bf16[2,1024,1024]{2,1,0:T(8,128)(2,1)}, f32[1024,256]{1,0:T(8,128)}) custom-call(f32[1024,1024]{1,0:T(8,128)} %raw.1, f32[1024,128]{1,0:T(8,128)} %broadcast_in_dim.12.rates_tall, f32[1,1024]{1,0:T(1,128)} %bitcast.8, f32[256,1024]{1,0:T(8,128)} %bitcast.9, f32[256,1024]{1,0:T(8,128)} %refs_5_.1, ...), custom_call_target="tpu_custom_call" | custom-call | flops 149999992832 | bytes 16777216 | tf_op jit(solution)/shard_map/chains/pallas_call | solution.py:341
  176.6 0.0 copy-start.2
  176.6 0.0 copy-start
  176.6 1.2 constant_dynamic-slice_fusion
  177.9 30.0 %collective-permute-start = (f32[512,256]{1,0:T(8,128)S(1)}, f32[512,256]{1,0:T(8,128)S(1)}, u32[]{:S(2)}, u32[]{:S(2)}) collective-permute-start(f32[512,256]{1,0:T(8,128)S(1)} %constant_dynamic-slice_fusion), channel_id=1, source_target_pairs={{0,4},{4,0},{8,12},{12,8},{16,20},{20,16},{24,28},{28,24},{1,5},{5... | collective-permute-start | bytes 1572872 | tf_op jit(solution)/shard_map/ppermute | solution.py:615
  207.8 0.0 copy-done.1
  207.9 0.1 dynamic_slice.16
  207.9 0.2 broadcast_add_fusion
  208.1 1.2 collective-permute-done
  209.4 1.5 multiply_add_fusion.2
  210.9 1.9 collective-permute-start.3
  212.8 1.3 collective-permute-start.2
  214.1 1.3 collective-permute-start.1
  215.4 0.0 copy-done.2
  215.4 7.0 %collective-permute-start.5 = (f32[256,1024]{1,0:T(8,128)S(1)}, f32[256,1024]{1,0:T(8,128)S(1)}, u32[]{:S(2)}, u32[]{:S(2)}) collective-permute-start(f32[256,1024]{1,0:T(8,128)S(1)} %bitcast.12), channel_id=1, source_target_pairs={{0,28},{4,0},{8,4},{12,8},{16,12},{20,16},{24,20},{28,24},{1,29},{... | collective-permute-start | bytes 3145736 | tf_op jit(solution)/shard_map/ppermute | solution.py:610
  222.4 3.7 %collective-permute-done.3 = f32[512,256]{1,0:T(8,128)S(1)} collective-permute-done((f32[512,256]{1,0:T(8,128)S(1)}, f32[512,256]{1,0:T(8,128)S(1)}, u32[]{:S(2)}, u32[]{:S(2)}) %collective-permute-start.3) | collective-permute-done | bytes 524320 | tf_op jit(solution)/shard_map/ppermute | solution.py:645
  226.1 11.1 %collective-permute-done.2 = f32[512,256]{1,0:T(8,128)S(1)} collective-permute-done((f32[512,256]{1,0:T(8,128)S(1)}, f32[512,256]{1,0:T(8,128)S(1)}, u32[]{:S(2)}, u32[]{:S(2)}) %collective-permute-start.2) | collective-permute-done | bytes 524320 | tf_op jit(solution)/shard_map/ppermute | solution.py:645
  237.3 5.0 %collective-permute-done.1 = f32[512,256]{1,0:T(8,128)S(1)} collective-permute-done((f32[512,256]{1,0:T(8,128)S(1)}, f32[512,256]{1,0:T(8,128)S(1)}, u32[]{:S(2)}, u32[]{:S(2)}) %collective-permute-start.1) | collective-permute-done | bytes 524320 | tf_op jit(solution)/shard_map/ppermute | solution.py:645
  242.3 0.0 copy-done
  242.3 0.3 broadcast_select_fusion.1
  242.6 0.1 collective-permute-start.4
  242.6 1.9 collective-permute-done.4
  244.5 0.1 maximum_select_fusion.refs_3_
  244.6 0.0 collective-permute-done.5.refs_4_
  244.7 82.8 %stages_3.1 = (f32[256,1024]{1,0:T(8,128)S(1)}, f32[256,1024]{1,0:T(8,128)S(1)}) custom-call(bf16[2,1024,1024]{2,1,0:T(8,128)(2,1)} %get-tuple-element.7.refs_0_, bf16[2,1024,1024]{2,1,0:T(8,128)(2,1)} %get-tuple-element.8.refs_1_, f32[1024,256]{1,0:T(8,128)S(1)} %get-tuple-element.15.refs_2_, f32[1024,256]{1,0:T(8,128)S(1)} %maximum_select_fusion.refs_3_, ...), custom_call_target="tpu_custom_call" | custom-call | flops 120000004096 | bytes 8388608 | tf_op jit(solution)/shard_map/stages_3/pallas_call | solution.py:578
  327.5 0.1 collective-permute-start.6
  327.6 20.3 %collective-permute-done.6 = f32[256,1024]{1,0:T(8,128)S(1)} collective-permute-done((f32[256,1024]{1,0:T(8,128)S(1)}, f32[256,1024]{1,0:T(8,128)S(1)}, u32[]{:S(2)}, u32[]{:S(2)}) %collective-permute-start.6) | collective-permute-done | bytes 1048608 | tf_op jit(solution)/shard_map/ppermute | solution.py:610
  347.9 1.0 copy.11
  348.8 1.0 copy.12
Async XLA Ops:
  2.3 205.5 %copy-start.1 = (f32[1024]{0:T(1024)S(1)}, f32[1024]{0:T(1024)}, u32[]{:S(2)}) copy-start(f32[1024]{0:T(1024)} %param.12) | copy-start | bytes 12292
  176.6 38.8 %copy-start.2 = (f32[1,256,1024]{2,1,0:T(8,128)S(1)}, f32[1,256,1024]{2,1,0:T(8,128)}, u32[]{:S(2)}) copy-start(f32[1,256,1024]{2,1,0:T(8,128)} %param.9) | copy-start | bytes 3145732
  176.6 65.7 %copy-start = (f32[1024,256]{1,0:T(8,128)S(1)}, f32[1024,256]{1,0:T(8,128)}, u32[]{:S(2)}) copy-start(f32[1024,256]{1,0:T(8,128)} %get-tuple-element.9) | copy-start | bytes 3145732
  177.9 31.5 %collective-permute-start = (f32[512,256]{1,0:T(8,128)S(1)}, f32[512,256]{1,0:T(8,128)S(1)}, u32[]{:S(2)}, u32[]{:S(2)}) collective-permute-start(f32[512,256]{1,0:T(8,128)S(1)} %constant_dynamic-slice_fusion), channel_id=1, source_target_pairs={{0,4},{4,0},{8,12},{12,8},{16,20},{20,16},{24,28},{28,24},{1,5},{5... | collective-permute-start | bytes 1572872 | tf_op jit(solution)/shard_map/ppermute | solution.py:615
  210.9 15.2 %collective-permute-start.3 = (f32[512,256]{1,0:T(8,128)S(1)}, f32[512,256]{1,0:T(8,128)S(1)}, u32[]{:S(2)}, u32[]{:S(2)}) collective-permute-start(f32[512,256]{1,0:T(8,128)S(1)} %multiply_add_fusion.2), channel_id=1, source_target_pairs={{24,0},{28,4},{0,8},{4,12},{8,16},{12,20},{16,24},{20,28},{25,1},{... | collective-permute-start | bytes 1572872 | tf_op jit(solution)/shard_map/ppermute | solution.py:645
  212.8 24.5 %collective-permute-start.2 = (f32[512,256]{1,0:T(8,128)S(1)}, f32[512,256]{1,0:T(8,128)S(1)}, u32[]{:S(2)}, u32[]{:S(2)}) collective-permute-start(f32[512,256]{1,0:T(8,128)S(1)} %multiply_add_fusion.2), channel_id=1, source_target_pairs={{24,8},{28,12},{0,16},{4,20},{8,24},{12,28},{25,9},{29,13},{1,17},... | collective-permute-start | bytes 1572872 | tf_op jit(solution)/shard_map/ppermute | solution.py:645
  214.1 28.2 %collective-permute-start.1 = (f32[512,256]{1,0:T(8,128)S(1)}, f32[512,256]{1,0:T(8,128)S(1)}, u32[]{:S(2)}, u32[]{:S(2)}) collective-permute-start(f32[512,256]{1,0:T(8,128)S(1)} %multiply_add_fusion.2), channel_id=1, source_target_pairs={{24,16},{28,20},{0,24},{4,28},{25,17},{29,21},{1,25},{5,29},{26,18... | collective-permute-start | bytes 1572872 | tf_op jit(solution)/shard_map/ppermute | solution.py:645
  215.4 29.2 %collective-permute-start.5 = (f32[256,1024]{1,0:T(8,128)S(1)}, f32[256,1024]{1,0:T(8,128)S(1)}, u32[]{:S(2)}, u32[]{:S(2)}) collective-permute-start(f32[256,1024]{1,0:T(8,128)S(1)} %bitcast.12), channel_id=1, source_target_pairs={{0,28},{4,0},{8,4},{12,8},{16,12},{20,16},{24,20},{28,24},{1,29},{... | collective-permute-start | bytes 3145736 | tf_op jit(solution)/shard_map/ppermute | solution.py:610
  242.6 2.0 collective-permute-start.4
  327.5 20.4 %collective-permute-start.6 = (f32[256,1024]{1,0:T(8,128)S(1)}, f32[256,1024]{1,0:T(8,128)S(1)}, u32[]{:S(2)}, u32[]{:S(2)}) collective-permute-start(f32[256,1024]{1,0:T(8,128)S(1)} %get-tuple-element.10), channel_id=1, source_target_pairs={{0,4},{4,8},{8,12},{12,16},{16,20},{20,24},{24,28},{28,0},{1,5},{5... | collective-permute-start | bytes 3145736 | tf_op jit(solution)/shard_map/ppermute | solution.py:610

commit v2 on v1

--- a/solution.py
+++ b/solution.py
@@ -24,14 +24,15 @@
 
 
 def chain_kernel(
-    raw, rates_tall, rates_wide, guess, initial, fine, coarse, basis, basis_t, terms,
-    before, entry, slots, field, coeffs, kept, wide, tall, part, sent, held, decay, coarse_decay, leaving, landed,
-    home_send, shift_recv, slot_recv, ex_send, ex_recv, term_send, term_recv,
+    raw, rates_tall, rates_wide, guess, initial, fine, coarse, basis, basis_t, terms, fine_next,
+    before, entry, coarse_next, slots, field, coeffs, kept, wide, tall, part, sent, held, decay, coarse_decay, leaving, landed,
+    home_send, shift_send, shift_recv, slot_recv, ex_send, ex_recv, term_send, term_recv,
 ):
     groups, count = lax.axis_size("tm"), lax.axis_size("space")
     t, s = lax.axis_index("tm"), lax.axis_index("space")
     grid = raw.shape[0]
     rows = fine.shape[0]
+    short = rows // 2
     half = grid // 2
     piece = half // 2
     per_half = count // 2
@@ -47,12 +48,10 @@
     def core(chain, which):
         return 2 * (chain // 2) + which
 
-    which = s // per_half
-    place = at((s % per_half) * rows, rows)
-    mine, past = t, (t + groups - 1) % groups
-    mine_at = (core(mine, which), seat(mine))
-    past_at = (core(past, which), seat(past))
-    to_self = (mine_at[0] == t) & (mine_at[1] == s)
+    position = s % per_half
+    group_at = (core(t, s // per_half), seat(t))
+    to_self = (group_at[0] == t) & (group_at[1] == s)
+    following, preceding = (t + 1) % groups, (t + groups - 1) % groups
 
     def remote(src, dst, send, recv, where):
         return pltpu.make_async_remote_copy(
@@ -60,29 +59,62 @@
             device_id={"tm": where[0], "space": where[1]}, device_id_type=MESH,
         )
 
-    def to_mine(src, slot, index):
-        pos = s % per_half
-        dst, recv = slots.at[slot, place], slot_recv.at[slot, pos]
+    def group_copy(src, slot, k):
+        part_of = src.at[at(k * short, short)]
+        dst = slots.at[slot, at(position * rows + k * short, short)]
+        return part_of, dst, home_send.at[slot, k], slot_recv.at[slot, 2 * position + k]
+
+    def to_group(src, slot, k):
+        part_of, dst, send, recv = group_copy(src, slot, k)
 
         @pl.when(jnp.logical_not(to_self))
         def _():
-            remote(src, dst, home_send.at[index], recv, mine_at).start()
+            remote(part_of, dst, send, recv, group_at).start()
 
         @pl.when(to_self)
         def _():
-            pltpu.make_async_copy(src, dst, recv).start()
-
-    def to_past(src, slot, index):
-        return remote(src, slots.at[slot, place], home_send.at[index], slot_recv.at[slot, s % per_half], past_at)
-
-    def pass_on():
-        return remote(guess, before, home_send.at[4], shift_recv.at[0], ((t + 1) % groups, s))
+            pltpu.make_async_copy(part_of, dst, recv).start()
+
+    def pass_on(index, src, dst, where):
+        return remote(src, dst, shift_send.at[index], shift_recv.at[index], (where, s))
+
+    pass_guess = pass_on(0, guess, before, following)
+    pass_fine = pass_on(1, fine, fine_next, preceding)
+    pass_entry = pass_on(1, entry, fine_next, preceding)
+    pass_coarse = pass_on(2, coarse, coarse_next, preceding)
 
     @pl.when(t != last)
     def _():
-        pass_on().start()
-
-    to_mine(coarse, 1, 0)
+        pass_guess.start()
+
+    @pl.when(t != 0)
+    def _():
+        pass_fine.start()
+
+    @pl.when(t == 0)
+    def _():
+        entry[...] = reacted(initial[...]) + fine[...]
+        pass_entry.start()
+
+    pass_coarse.start()
+
+    @pl.when(t % 2 == 0)
+    def _():
+        to_group(coarse, 1, 0)
+
+    @pl.when(t != 0)
+    def _():
+        pass_guess.wait_recv()
+        entry[...] = reacted(before[...]) + fine[...]
+
+    to_group(entry, 0, 0)
+    to_group(entry, 0, 1)
+
+    @pl.when(t % 2 == 1)
+    def _():
+        to_group(coarse, 1, 0)
+
+    to_group(coarse, 1, 1)
 
     @pl.loop(0, count)
     def _(r):
@@ -90,26 +122,12 @@
         basis[0, at(r * rows, rows), :] = high
         basis[1, at(r * rows, rows), :] = low
 
-    @pl.when(t != 0)
-    def _():
-        remote(guess, before, home_send.at[4], shift_recv.at[0], (t, s)).wait_recv()
-        entry[...] = reacted(before[...]) + fine[...]
-
-    @pl.when(t == 0)
-    def _():
-        entry[...] = reacted(initial[...]) + fine[...]
-
-    to_mine(entry, 0, 1)
-
-    @pl.when(t == 0)
-    def _():
-        to_past(entry, 2, 2).start()
-
-    @pl.when(t != 0)
-    def _():
-        to_past(fine, 2, 2).start()
-
-    to_past(coarse, 3, 3).start()
+    pass_fine.wait_recv()
+    to_group(fine_next, 2, 0)
+    to_group(fine_next, 2, 1)
+    pass_coarse.wait_recv()
+    to_group(coarse_next, 3, 0)
+    to_group(coarse_next, 3, 1)
 
     @pl.loop(0, grid // piece)
     def _(r):
@@ -121,25 +139,22 @@
 
     side = t % 2
     group = 2 * (t // 2) + (s - low_seat)
-    partner = (2 * (t // 2) + 1 - side, s)
+    partner = (core(t, 1 - side), s)
     own, other = at(side * half, half), at((1 - side) * half, half)
 
-    def wait_slot(slot, position):
-        source = side * per_half + position
-        dst, recv = slots.at[slot, at(position * rows, rows)], slot_recv.at[slot, position]
-        local = (group == t) & (source == s) if slot < 2 else None
-
-        def arrive():
-            remote(fine, dst, home_send.at[0], recv, (t, s)).wait_recv()
-
-        if local is None:
-            arrive()
-        else:
-            pl.when(jnp.logical_not(local))(arrive)
+    def wait_slot(slot, index):
+        local = (group == t) & (side * per_half + index == s)
+        for k in range(2):
+            dst = slots.at[slot, at(index * rows + k * short, short)]
+            src, recv = fine.at[at(k * short, short)], slot_recv.at[slot, 2 * index + k]
+
+            @pl.when(jnp.logical_not(local))
+            def _():
+                remote(src, dst, home_send.at[slot, k], recv, (t, s)).wait_recv()
 
             @pl.when(local)
             def _():
-                pltpu.make_async_copy(fine, dst, recv).wait()
+                pltpu.make_async_copy(src, dst, recv).wait()
 
     def exchange(stage, m):
         block = at(m * piece, piece)
@@ -311,15 +326,16 @@
 
     @pl.when(jnp.logical_not(to_self))
     def _():
-        for index, src in ((0, coarse), (1, entry)):
-            remote(src, slots.at[0, place], home_send.at[index], slot_recv.at[0, 0], mine_at).wait_send()
-
-    for index in (2, 3):
-        remote(fine, slots.at[0, place], home_send.at[index], slot_recv.at[0, 0], past_at).wait_send()
+        for slot, src in enumerate((entry, coarse, fine_next, coarse_next)):
+            for k in range(2):
+                remote(*group_copy(src, slot, k), group_at).wait_send()
 
     @pl.when(t != last)
     def _():
-        pass_on().wait_send()
+        pass_guess.wait_send()
+
+    pass_fine.wait_send()
+    pass_coarse.wait_send()
 
 
 def chains(basis, rates, guess, initial, fine, coarse):
@@ -335,6 +351,7 @@
         jax.ShapeDtypeStruct((2, grid, grid), bf16),
         jax.ShapeDtypeStruct((2, grid, grid), bf16),
         jax.ShapeDtypeStruct((grid, rows), f32),
+        jax.ShapeDtypeStruct((rows, grid), f32),
     ]
     vmem = pl.BlockSpec(memory_space=pltpu.VMEM)
     dma = pltpu.SemaphoreType.DMA
@@ -344,6 +361,7 @@
         in_specs=[vmem] * len(operands),
         out_specs=[vmem] * len(shapes),
         scratch_shapes=[
+            pltpu.VMEM((rows, grid), f32),
             pltpu.VMEM((rows, grid), f32),
             pltpu.VMEM((rows, grid), f32),
             pltpu.VMEM((4, half, grid), f32),
@@ -359,9 +377,10 @@
             pltpu.VMEM((grid, half), f32),
             pltpu.VMEM((per_half, grid, rows), f32),
             pltpu.VMEM((grid, rows), f32),
-            dma((5,)),
-            dma((1,)),
-            dma((4, per_half)),
+            dma((4, 2)),
+            dma((3,)),
+            dma((3,)),
+            dma((4, count)),
             dma((steps, 2)),
             dma((steps, 2)),
             dma((per_half, grid // piece)),
@@ -506,7 +525,8 @@
 
     def react(source):
         value = field[...]
-        field[...] = value + 0.5 * jnp.tanh(value) + source[...]
+        moved = jnp.where(lax.axis_index("tm") == lax.axis_size("tm") - 1, 0.0, value + 0.5 * jnp.tanh(value))
+        field[...] = moved + source[...]
 
     sources = list(sources)
     outs = list(outs)
@@ -529,10 +549,6 @@
             if stage in forced:
                 outs.pop(0)[...] = field[...]
             if not final:
-                if fixed is not None:
-                    @pl.when(lax.axis_index("tm") == lax.axis_size("tm") - 1)
-                    def _():
-                        field[...] = fixed[...]
                 react(sources.pop(0))
 
     for stage in range(len(plan)):
@@ -673,13 +689,12 @@
     coarse_decay = decay_block(eigen_rates, own_rates, 2.0)
     carried = lax.dynamic_slice_in_dim(carried_correction, offset, row_count, 1)
     place = lax.axis_index("tm")
-    basis, basis_t, terms = chains(
+    basis, basis_t, terms, fine_next = chains(
         eigen_basis, eigen_rates, guess_coarse[0], initial_state, force_fine[0], force_coarse[0]
     )
-    fine_next = shift(force_fine[0], -1)
     states = coarse_solve(terms, carried, coarse_decay)
     coarse_new, fine_new = stages(
-        "IEI", (0, 2), 3, basis=(basis, basis_t), decay=fine_decay, start=states, sources=[fine_next], fixed=initial_state
+        "IEI", (0, 2), 3, basis=(basis, basis_t), decay=fine_decay, start=states, sources=[fine_next]
     )
     return (shift(fine_new, 1)[None], coarse_new[None])
 

time: 355 us -> 291 us (0.82); the launches traced: 350 us -> 290 us
  starting transfers between devices: 41.7 us -> 10.6 us
  Pallas kernels: 257 us -> 230 us
    pallas_call x1, Pallas kernels: 174 us -> 150 us  [chains(): pl.pallas_call(chain_kernel, out_shape=shapes, in_specs=[vmem] * len(oper...]
    ppermute x2, starting transfers between devices: 30.1 us -> 7.87 us  [swap(): return lax.ppermute(block, 'tm', [(i, i ^ 1) for i in range(count)])]
    ppermute x2 -> x1, starting transfers between devices: 7.12 us -> 0.11 us  [shift(): lax.ppermute(block, 'tm', [(i, (i + distance) % count) for i in range(cou...]
    ppermute x2 -> x1, waiting for transfers between devices: 20.3 us -> 15.1 us  [shift(): lax.ppermute(block, 'tm', [(i, (i + distance) % count) for i in range(cou...]
    ppermute x3, waiting for transfers between devices: 19.9 us -> 23.7 us  [coarse_solve(): arrived[s] = lax.ppermute(sums, 'tm', route)]
  transfers between devices with their start and end apart: 7 -> 6, of which waited for: 6 -> 5; matrix products, arithmetic and copies ran while one was open for 0% -> 0% of each run, Pallas kernels for 0% -> 0%
where the time goes in v2:
time: 291 us; the launch traced here: 290 us
  Pallas kernels  230 us (79%)
  waiting for transfers between devices  41.9 us (14%)
  starting transfers between devices  10.6 us (4%)
  local copies, waits for them, and re-layouts  4.88 us (2%)
    pallas_call x1, Pallas kernels, chains(): pl.pallas_call(chain_kernel, out_shape=shapes, in_specs=[vmem] * len(oper...  150 us
    pallas_call x1, Pallas kernels, stages(): pl.pallas_call(kernel, out_shape=shapes, in_specs=[vmem] * len(operands),...  80 us
    ppermute x3, waiting for transfers between devices, coarse_solve(): arrived[s] = lax.ppermute(sums, 'tm', route)  23.7 us
    ppermute x1, waiting for transfers between devices, shift(): lax.ppermute(block, 'tm', [(i, (i + distance) % count) for i in range(cou...  15.1 us
    ppermute x2, starting transfers between devices, swap(): return lax.ppermute(block, 'tm', [(i, i ^ 1) for i in range(count)])  7.87 us
  transfers between devices with their start and end apart: 6, of which 5 were waited for; matrix products, arithmetic and copies ran while one was open for 0% of the time, Pallas kernels for 0%

profile of v2, /device:TPU:12, one launch (start us, length us, event | category | flops | bytes accessed | tf_op | source)
XLA Modules:
  0.0 290.0 jit_solution(16748573324417512700)
XLA Ops:
  0.7 1.7 broadcast_in_dim.12.rates_tall
  2.3 0.0 copy-start.2
  2.3 149.7 %chains.1 = (bf16[2,1024,1024]{2,1,0:T(8,128)(2,1)}, bf16[2,1024,1024]{2,1,0:T(8,128)(2,1)}, f32[1024,256]{1,0:T(8,128)}, f32[256,1024]{1,0:T(8,128)}) custom-call(f32[1024,1024]{1,0:T(8,128)} %raw.1, f32[1024,128]{1,0:T(8,128)} %broadcast_in_dim.12.rates_tall, f32[1,1024]{1,0:T(1,128)} %bitcast.8, f32[256,1024]{1,0:T(8,128)} %bitcast.9, ...), custom_call_target="tpu_custom_call" | custom-call | flops 149999992832 | bytes 16777216 | tf_op jit(solution)/shard_map/chains/pallas_call | solution.py:358
  152.1 0.0 copy-start.1
  152.1 1.2 constant_dynamic-slice_fusion
  153.3 7.7 %collective-permute-start = (f32[512,256]{1,0:T(8,128)S(1)}, f32[512,256]{1,0:T(8,128)S(1)}, u32[]{:S(2)}, u32[]{:S(2)}) collective-permute-start(f32[512,256]{1,0:T(8,128)S(1)} %constant_dynamic-slice_fusion), channel_id=1, source_target_pairs={{0,4},{4,0},{8,12},{12,8},{16,20},{20,16},{24,28},{28,24},{1,5},{5... | collective-permute-start | bytes 1572872 | tf_op jit(solution)/shard_map/ppermute | solution.py:631
  161.0 0.0 copy-done.2
  161.0 0.1 dynamic_slice.16
  161.1 0.2 broadcast_add_fusion
  161.3 1.2 collective-permute-done
  162.5 0.0 copy-start
  162.5 1.6 multiply_add_fusion.2
  164.1 0.1 collective-permute-start.3
  164.2 1.3 collective-permute-start.2
  165.5 1.3 collective-permute-start.1
  166.8 12.6 %collective-permute-done.3 = f32[512,256]{1,0:T(8,128)S(1)} collective-permute-done((f32[512,256]{1,0:T(8,128)S(1)}, f32[512,256]{1,0:T(8,128)S(1)}, u32[]{:S(2)}, u32[]{:S(2)}) %collective-permute-start.3) | collective-permute-done | bytes 524320 | tf_op jit(solution)/shard_map/ppermute | solution.py:661
  179.4 11.1 %collective-permute-done.2 = f32[512,256]{1,0:T(8,128)S(1)} collective-permute-done((f32[512,256]{1,0:T(8,128)S(1)}, f32[512,256]{1,0:T(8,128)S(1)}, u32[]{:S(2)}, u32[]{:S(2)}) %collective-permute-start.2) | collective-permute-done | bytes 524320 | tf_op jit(solution)/shard_map/ppermute | solution.py:661
  190.5 0.0 collective-permute-done.1
  190.5 0.0 copy-done.1
  190.5 0.3 broadcast_select_fusion.1
  190.8 0.1 collective-permute-start.4
  190.9 1.8 collective-permute-done.4
  192.8 0.1 maximum_select_fusion.refs_3_
  192.9 0.0 copy-done
  192.9 80.0 %stages_3.1 = (f32[256,1024]{1,0:T(8,128)S(1)}, f32[256,1024]{1,0:T(8,128)S(1)}) custom-call(bf16[2,1024,1024]{2,1,0:T(8,128)(2,1)} %get-tuple-element.8.refs_0_, bf16[2,1024,1024]{2,1,0:T(8,128)(2,1)} %get-tuple-element.9.refs_1_, f32[1024,256]{1,0:T(8,128)S(1)} %get-tuple-element.17.refs_2_, f32[1024,256]{1,0:T(8,128)S(1)} %maximum_select_fusion.refs_3_, ...), custom_call_target="tpu_custom_call" | custom-call | flops 120000004096 | bytes 8388608 | tf_op jit(solution)/shard_map/stages_3/pallas_call | solution.py:594
  272.9 0.1 collective-permute-start.5
  273.0 15.1 %collective-permute-done.5 = f32[256,1024]{1,0:T(8,128)S(1)} collective-permute-done((f32[256,1024]{1,0:T(8,128)S(1)}, f32[256,1024]{1,0:T(8,128)S(1)}, u32[]{:S(2)}, u32[]{:S(2)}) %collective-permute-start.5) | collective-permute-done | bytes 1048608 | tf_op jit(solution)/shard_map/ppermute | solution.py:626
  288.1 1.0 copy.11
  289.0 1.0 copy.12
Async XLA Ops:
  2.3 158.7 %copy-start.2 = (f32[1024]{0:T(1024)S(1)}, f32[1024]{0:T(1024)}, u32[]{:S(2)}) copy-start(f32[1024]{0:T(1024)} %param.12) | copy-start | bytes 12292
  152.1 38.5 %copy-start.1 = (f32[1024,256]{1,0:T(8,128)S(1)}, f32[1024,256]{1,0:T(8,128)}, u32[]{:S(2)}) copy-start(f32[1024,256]{1,0:T(8,128)} %get-tuple-element.10) | copy-start | bytes 3145732
  153.3 9.3 %collective-permute-start = (f32[512,256]{1,0:T(8,128)S(1)}, f32[512,256]{1,0:T(8,128)S(1)}, u32[]{:S(2)}, u32[]{:S(2)}) collective-permute-start(f32[512,256]{1,0:T(8,128)S(1)} %constant_dynamic-slice_fusion), channel_id=1, source_target_pairs={{0,4},{4,0},{8,12},{12,8},{16,20},{20,16},{24,28},{28,24},{1,5},{5... | collective-permute-start | bytes 1572872 | tf_op jit(solution)/shard_map/ppermute | solution.py:631
  162.5 30.4 %copy-start = (f32[256,1024]{1,0:T(8,128)S(1)}, f32[256,1024]{1,0:T(8,128)}, u32[]{:S(2)}) copy-start(f32[256,1024]{1,0:T(8,128)} %get-tuple-element.11.refs_4_) | copy-start | bytes 3145732
  164.1 15.2 %collective-permute-start.3 = (f32[512,256]{1,0:T(8,128)S(1)}, f32[512,256]{1,0:T(8,128)S(1)}, u32[]{:S(2)}, u32[]{:S(2)}) collective-permute-start(f32[512,256]{1,0:T(8,128)S(1)} %multiply_add_fusion.2), channel_id=1, source_target_pairs={{24,0},{28,4},{0,8},{4,12},{8,16},{12,20},{16,24},{20,28},{25,1},{... | collective-permute-start | bytes 1572872 | tf_op jit(solution)/shard_map/ppermute | solution.py:661
  164.2 26.3 %collective-permute-start.2 = (f32[512,256]{1,0:T(8,128)S(1)}, f32[512,256]{1,0:T(8,128)S(1)}, u32[]{:S(2)}, u32[]{:S(2)}) collective-permute-start(f32[512,256]{1,0:T(8,128)S(1)} %multiply_add_fusion.2), channel_id=1, source_target_pairs={{24,8},{28,12},{0,16},{4,20},{8,24},{12,28},{25,9},{29,13},{1,17},... | collective-permute-start | bytes 1572872 | tf_op jit(solution)/shard_map/ppermute | solution.py:661
  165.5 25.0 %collective-permute-start.1 = (f32[512,256]{1,0:T(8,128)S(1)}, f32[512,256]{1,0:T(8,128)S(1)}, u32[]{:S(2)}, u32[]{:S(2)}) collective-permute-start(f32[512,256]{1,0:T(8,128)S(1)} %multiply_add_fusion.2), channel_id=1, source_target_pairs={{24,16},{28,20},{0,24},{4,28},{25,17},{29,21},{1,25},{5,29},{26,18... | collective-permute-start | bytes 1572872 | tf_op jit(solution)/shard_map/ppermute | solution.py:661
  190.8 2.0 collective-permute-start.4
  272.9 15.2 %collective-permute-start.5 = (f32[256,1024]{1,0:T(8,128)S(1)}, f32[256,1024]{1,0:T(8,128)S(1)}, u32[]{:S(2)}, u32[]{:S(2)}) collective-permute-start(f32[256,1024]{1,0:T(8,128)S(1)} %get-tuple-element.12), channel_id=1, source_target_pairs={{0,4},{4,8},{8,12},{12,16},{16,20},{20,24},{24,28},{28,0},{1,5},{5... | collective-permute-start | bytes 3145736 | tf_op jit(solution)/shard_map/ppermute | solution.py:626

commit v3 on v2

v3 whole, which is shorter than its diff:
```python
import functools
import jax
import jax.numpy as jnp
from jax import lax
from jax.experimental import pallas as pl
from jax.experimental.pallas import tpu as pltpu
from jax.sharding import PartitionSpec as P

MESH = pl.DeviceIdType.MESH


def halves(block):
    high = block.astype(jnp.bfloat16)
    return high, (block - high.astype(jnp.float32)).astype(jnp.bfloat16)


def dot3(left, right):
    dot = functools.partial(jnp.dot, preferred_element_type=jnp.float32)
    return dot(left[0], right[0]) + dot(left[0], right[1]) + dot(left[1], right[0])


def reacted(value):
    return value + 0.5 * jnp.tanh(value)


def cycle_kernel(
    raw, rates, guess, initial, fine, coarse, carried, fine_out, coarse_out,
    basis, basis_t, rates_tall, before, entry, fine_next, coarse_next, slots, field, coeffs, kept, wide, tall, part,
    sent, held, decay, landed, joined, gathered, evens, got, crossed, start,
    home_send, shift_send, shift_recv, slot_recv, ex_send, ex_recv, term_send, term_recv,
    pair_send, pair_recv, share_send, share_recv, cross_send, cross_recv, start_sem,
):
    groups, count = lax.axis_size("tm"), lax.axis_size("space")
    t, s = lax.axis_index("tm"), lax.axis_index("space")
    grid = raw.shape[0]
    rows = fine.shape[0]
    short = rows // 2
    half = grid // 2
    piece = half // 2
    pieces = grid // piece
    per_half = count // 2
    low_seat = per_half - 1
    last = groups - 1
    lanes = rates_tall.shape[1]
    cuts = rows // lanes
    pairs = groups // 2
    share = half // pairs

    def at(start, size):
        return pl.ds(pl.multiple_of(start, size), size)

    def span(d):
        return at(d * rows, rows)

    def seat(chain):
        return low_seat + chain % 2

    def core(chain, which):
        return 2 * (chain // 2) + which

    def remote(src, dst, send, recv, where):
        return pltpu.make_async_remote_copy(
            src_ref=src, dst_ref=dst, send_sem=send, recv_sem=recv,
            device_id={"tm": where[0], "space": where[1]}, device_id_type=MESH,
        )

    position = s % per_half
    group_at = (core(t, s // per_half), seat(t))
    to_self = (group_at[0] == t) & (group_at[1] == s)
    following, preceding = (t + 1) % groups, (t + groups - 1) % groups

    def group_copy(src, slot, k):
        part_of = src.at[at(k * short, short)]
        dst = slots.at[slot, at(position * rows + k * short, short)]
        return part_of, dst, home_send.at[slot, k], slot_recv.at[slot, 2 * position + k]

    def to_group(src, slot, k):
        part_of, dst, send, recv = group_copy(src, slot, k)

        @pl.when(jnp.logical_not(to_self))
        def _():
            remote(part_of, dst, send, recv, group_at).start()

        @pl.when(to_self)
        def _():
            pltpu.make_async_copy(part_of, dst, recv).start()

    def pass_on(index, src, dst, where):
        return remote(src, dst, shift_send.at[index], shift_recv.at[index], (where, s))

    pass_guess = pass_on(0, guess, before, following)
    pass_fine = pass_on(1, fine, fine_next, preceding)
    pass_entry = pass_on(1, entry, fine_next, preceding)
    pass_coarse = pass_on(2, coarse, coarse_next, preceding)

    side = t % 2
    pair = t // 2
    own, other = at(side * half, half), at((1 - side) * half, half)
    partner = (core(t, 1 - side), s)
    start_copy = pltpu.make_async_copy(
        carried.at[at(side * half + pair * share, share), span(s)], start, start_sem.at[0]
    )

    @pl.when(t != last)
    def _():
        pass_guess.start()

    @pl.when(t != 0)
    def _():
        pass_fine.start()

    @pl.when(t == 0)
    def _():
        entry[...] = reacted(initial[...]) + fine[...]
        pass_entry.start()

    pass_coarse.start()
    start_copy.start()

    @pl.when(t % 2 == 0)
    def _():
        to_group(coarse, 1, 0)

    @pl.when(t != 0)
    def _():
        pass_guess.wait_recv()
        entry[...] = reacted(before[...]) + fine[...]

    to_group(entry, 0, 0)
    to_group(entry, 0, 1)

    @pl.when(t % 2 == 1)
    def _():
        to_group(coarse, 1, 0)

    to_group(coarse, 1, 1)

    @pl.loop(0, count)
    def _(r):
        high, low = halves(raw[span(r), :])
        basis[0, span(r), :] = high
        basis[1, span(r), :] = low

    pass_fine.wait_recv()
    to_group(fine_next, 2, 0)
    to_group(fine_next, 2, 1)
    pass_coarse.wait_recv()
    to_group(coarse_next, 3, 0)
    to_group(coarse_next, 3, 1)

    @pl.loop(0, pieces)
    def _(r):
        @pl.loop(0, pieces)
        def _(c):
            high, low = halves(raw[at(c * piece, piece), at(r * piece, piece)].T)
            basis_t[0, at(r * piece, piece), at(c * piece, piece)] = high
            basis_t[1, at(r * piece, piece), at(c * piece, piece)] = low

    @pl.loop(0, grid // lanes)
    def _(r):
        rates_tall[at(r * lanes, lanes), :] = jnp.broadcast_to(rates[:, at(r * lanes, lanes)], (lanes, lanes)).T

    def sums_of_rates(block, columns):
        return rates_tall[block, :1] + rates[:, columns]

    def fine_decay(block, columns):
        return 1.0 / (1.0 + sums_of_rates(block, columns))

    def coarse_decay(block, columns):
        return 1.0 / (1.0 + 2.0 * sums_of_rates(block, columns))

    group = core(t, s - low_seat)

    def wait_slot(slot, index):
        local = (group == t) & (side * per_half + index == s)
        for k in range(2):
            dst = slots.at[slot, at(index * rows + k * short, short)]
            src, recv = fine.at[at(k * short, short)], slot_recv.at[slot, 2 * index + k]

            @pl.when(jnp.logical_not(local))
            def _():
                remote(src, dst, home_send.at[slot, k], recv, (t, s)).wait_recv()

            @pl.when(local)
            def _():
                pltpu.make_async_copy(src, dst, recv).wait()

    def exchange(stage, m):
        block = at(m * piece, piece)
        return remote(sent.at[stage % 2, block], held.at[stage % 2, block], ex_send.at[stage, m], ex_recv.at[stage, m], partner)

    def halves_to(ref, index, value):
        ref[(0, *index)], ref[(1, *index)] = halves(value)

    def reorder(value, order):
        if not order:
            return value
        return jnp.concatenate(
            [value[:, q * rows + h * lanes:q * rows + (h + 1) * lanes] for h in range(cuts) for q in range(per_half)], 1
        )

    def collect(stage, into, order=False):
        for m in range(2):
            block = at(m * piece, piece)
            exchange(stage, m).wait_recv()
            halves_to(into, (block, slice(0, half)), reorder(held[stage % 2, block, :], order))

    def free(stage):
        if stage >= 2:
            for m in range(2):
                exchange(stage - 2, m).wait_send()

    def right_of(stage, source, slot, order=False):
        free(stage)
        for m in range(2):
            block = at(m * piece, piece)
            for index in range(m * per_half // 2, (m + 1) * per_half // 2):
                wait_slot(slot, index)
            halves_to(wide, (block, slice(None)), source(block))
            left = (wide[0, block, :], wide[1, block, :])
            sent[stage % 2, block] = dot3(left, (basis[0, :, other], basis[1, :, other]))
            exchange(stage, m).start()
            halves_to(part, (block, slice(None)), reorder(dot3(left, (basis[0, :, own], basis[1, :, own])), order))

    def forward(stage, source, slot, finish):
        right_of(stage, source, slot)

        @pl.loop(0, 2)
        def _(n):
            columns = at(n * piece, piece)
            coeffs[:, columns] = dot3((basis_t[0, :, own], basis_t[1, :, own]), (part[0, :, columns], part[1, :, columns]))

        collect(stage, part)

        @pl.loop(0, 2)
        def _(n):
            columns = at(n * piece, piece)
            term = dot3((basis_t[0, :, other], basis_t[1, :, other]), (part[0, :, columns], part[1, :, columns]))
            value = (coeffs[:, columns] + term) * decay[:, columns]
            coeffs[:, columns] = value
            finish(n, columns, value)

    def inverse(stage):
        free(stage)

        @pl.loop(0, pieces)
        def _(r):
            block = at(r * piece, piece)
            halves_to(tall, (block, slice(None)), coeffs[block, :])

        def rows_of(m, which):
            block = at(which * half + m * piece, piece)
            return dot3((basis[0, block, :], basis[1, block, :]), (tall[0], tall[1]))

        @pl.loop(0, 2)
        def _(m):
            sent[stage % 2, at(m * piece, piece)] = rows_of(m, 1 - side)
            exchange(stage, m).start()

        @pl.loop(0, 2)
        def _(m):
            halves_to(part, (at(m * piece, piece), slice(None)), rows_of(m, side))

        @pl.loop(0, 2)
        def _(n):
            columns = at(n * half, half)
            field[:, columns] = dot3((part[0], part[1]), (basis_t[0, own, columns], basis_t[1, own, columns]))

        collect(stage, part)

        @pl.loop(0, 2)
        def _(n):
            columns = at(n * half, half)
            field[:, columns] = field[:, columns] + dot3(
                (part[0], part[1]), (basis_t[0, other, columns], basis_t[1, other, columns])
            )

    def term_place(q):
        return group, side * per_half + q

    def term_refs(h, r, q):
        block = at(r * piece, piece)
        source = coeffs.at[block, at((h * per_half + q) * lanes, lanes)]
        return source, landed.at[block, at(h * lanes, lanes)]

    def term_here(q):
        where = term_place(q)
        return (where[0] == t) & (where[1] == s)

    def send_term(h, r, q):
        source, target = term_refs(h, r, q)

        @pl.when(term_here(q))
        def _():
            pltpu.make_async_copy(source, target, term_recv.at[h, r]).start()

        @pl.when(jnp.logical_not(term_here(q)))
        def _():
            remote(source, target, term_send.at[h, r, q], term_recv.at[h, r], term_place(q)).start()

    @pl.when((s == low_seat) | (s == low_seat + 1))
    def _():
        @pl.loop(0, pieces)
        def _(r):
            block = at(r * piece, piece)
            decay[block, :] = fine_decay(block, own)

        def plain(n, columns, value):
            pass

        def keep(n, columns, value):
            taken = value * coarse_decay(slice(None), at(side * half + n * piece, piece))
            kept[:, columns] = jnp.where(group == last, 0.0, taken)

        def from_field(slot):
            def source(block):
                moved = reacted(field[block, :])
                if slot == 2:
                    moved = jnp.where(group == last, 0.0, moved)
                return moved + slots[slot, block, :]
            return source

        forward(0, lambda block: slots[0, block, :], 0, plain)
        inverse(1)
        forward(2, from_field(1), 1, keep)
        inverse(3)
        forward(4, from_field(2), 2, plain)
        inverse(5)

        right_of(6, from_field(3), 3, True)
        collect(6, wide, True)
        for h in range(cuts):
            columns = slice(h * per_half * lanes, (h + 1) * per_half * lanes)

            @pl.loop(0, pieces)
            def _(r):
                block = at(r * piece, piece)
                value = dot3((basis_t[0, block, own], basis_t[1, block, own]), (part[0, :, columns], part[1, :, columns]))
                value = value + dot3(
                    (basis_t[0, block, other], basis_t[1, block, other]), (wide[0, :, columns], wide[1, :, columns])
                )
                for q in range(per_half):
                    natural = slice(q * rows + h * lanes, q * rows + (h + 1) * lanes)
                    coeffs[block, at((h * per_half + q) * lanes, lanes)] = (
                        value[:, q * lanes:(q + 1) * lanes] * decay[block, natural] - kept[block, natural]
                    )
                for q in range(per_half):
                    send_term(h, r, q)

        for stage in (5, 6):
            for m in range(2):
                exchange(stage, m).wait_send()

    sender = (core(t, s // per_half), seat(t))
    from_self = (sender[0] == t) & (sender[1] == s)

    def wait_term(h, r):
        source, target = term_refs(h, r, 0)

        @pl.when(from_self)
        def _():
            pltpu.make_async_copy(source, target, term_recv.at[h, r]).wait()

        @pl.when(jnp.logical_not(from_self))
        def _():
            remote(source, target, term_send.at[h, r, 0], term_recv.at[h, r], (t, s)).wait_recv()

    spread, fanned, given = (slots.at[0, :, at(k * rows, rows)] for k in range(3))

    def cut(h):
        return at(h * lanes, lanes)

    def column_of(h):
        return at(s * rows + h * lanes, lanes)

    def swap_terms(h):
        return remote(landed.at[other, cut(h)], joined.at[:, cut(h)], pair_send.at[0, h], pair_recv.at[0, h], partner)

    def swap_states(h):
        return remote(given.at[:, cut(h)], got.at[:, cut(h)], pair_send.at[1, h], pair_recv.at[1, h], partner)

    def share_out(h, k):
        return remote(
            spread.at[at(k * share, share), cut(h)], gathered.at[pair, :, cut(h)],
            share_send.at[0, h, k], share_recv.at[0, h, pair], (core(2 * k, side), s),
        )

    def share_in(h, k):
        return remote(
            spread.at[at(k * share, share), cut(h)], gathered.at[k, :, cut(h)],
            share_send.at[0, h, k], share_recv.at[0, h, k], (core(2 * k, side), s),
        )

    def fan_out(h, k):
        return remote(
            fanned.at[at(k * share, share), cut(h)], evens.at[at(pair * share, share), cut(h)],
            share_send.at[1, h, k], share_recv.at[1, h, pair], (core(2 * k, side), s),
        )

    def fan_in(h, k):
        return remote(
            fanned.at[at(k * share, share), cut(h)], evens.at[at(k * share, share), cut(h)],
            share_send.at[1, h, k], share_recv.at[1, h, k], (core(2 * k, side), s),
        )

    def elsewhere(act):
        @pl.loop(0, pairs)
        def _(k):
            @pl.when(k != pair)
            def _():
                act(k)

    def solve(h):
        for r in range(pieces):
            wait_term(h, r)
        swap_terms(h).start()
        rate = coarse_decay(own, column_of(h))
        swap_terms(h).wait_recv()
        mine, theirs = landed[own, cut(h)], joined[:, cut(h)]
        first = jnp.where(side == 0, mine, theirs)
        second = jnp.where(side == 0, theirs, mine)
        spread[:, cut(h)] = second + jnp.where(pair == pairs - 1, 0.0, rate * first)
        elsewhere(lambda k: share_out(h, k).start())
        gathered[pair, :, cut(h)] = spread[at(pair * share, share), cut(h)]
        if h == 0:
            start_copy.wait()
        elsewhere(lambda k: share_in(h, k).wait_recv())
        near = coarse_decay(at(side * half + pair * share, share), column_of(h))
        value = gathered[pairs - 1, :, cut(h)] + near * start[:, cut(h)]
        fanned[0:share, cut(h)] = value
        near = near * near
        for k in range(pairs - 1):
            value = gathered[k, :, cut(h)] + near * value
            fanned[(k + 1) * share:(k + 2) * share, cut(h)] = value
        elsewhere(lambda k: fan_out(h, k).start())
        evens[at(pair * share, share), cut(h)] = fanned[at(pair * share, share), cut(h)]
        elsewhere(lambda k: fan_in(h, k).wait_recv())
        even = evens[:, cut(h)]
        odd = first + rate * even
        given[:, cut(h)] = jnp.where(side == 0, odd, even)
        swap_states(h).start()
        halves_to(tall, (own, cut(h)), jnp.where(side == 0, even, odd))
        swap_states(h).wait_recv()
        halves_to(tall, (other, cut(h)), got[:, cut(h)])

    def peer(k):
        return jnp.where(s < count // 2, count - 1 - k, k)

    def cross(stage, d, h, width, to, by):
        window = pl.ds(pl.multiple_of(d * rows + h * width, width), width)
        return remote(
            slots.at[stage + 1, 0:rows, window], crossed.at[stage, by, :, at(h * width, width)],
            cross_send.at[stage, d, h], cross_recv.at[stage, by, h], (to, d),
        )

    def dispatch(stage, h, width, block_for, to, keeps):
        @pl.loop(0, count)
        def _(k):
            d = peer(k)
            block = block_for(d)

            def away():
                slots[stage + 1, 0:rows, pl.ds(pl.multiple_of(d * rows + h * width, width), width)] = block
                cross(stage, d, h, width, to, s).start()

            if keeps:
                pl.when(d != s)(away)

                @pl.when(d == s)
                def _():
                    crossed[stage, s, :, at(h * width, width)] = block
            else:
                away()

    def absorb(stage, parts, width, use, keeps):
        if keeps:
            use(s, True)

        @pl.loop(0, count)
        def _(k):
            d = peer(k)

            def arrive(first):
                for h in range(parts):
                    cross(stage, d, h, width, t, d).wait_recv()
                use(d, first)

            if keeps:
                pl.when(d != s)(lambda: arrive(False))
            else:
                pl.when(k == 0)(lambda: arrive(True))
                pl.when(k != 0)(lambda: arrive(False))

    def left_rows(d, columns):
        return dot3((basis[0, span(d), :], basis[1, span(d), :]), (tall[0, :, columns], tall[1, :, columns]))

    def rows_into(ref, stage):
        def use(d, first):
            block = halves(crossed[stage, d])

            @pl.loop(0, 2)
            def _(n):
                columns = at(n * half, half)
                term = dot3(block, (basis_t[0, span(d), columns], basis_t[1, span(d), columns]))
                ref[:, columns] = term if first else ref[:, columns] + term
        return use

    for h in range(cuts):
        solve(h)
        dispatch(0, h, lanes, lambda d: left_rows(d, slice(h * lanes, (h + 1) * lanes)), t, True)

    absorb(0, cuts, lanes, rows_into(coarse_out, 0), True)
    moved = jnp.where(t == last, 0.0, reacted(coarse_out[...]))
    halves_to(wide, (slice(0, rows), slice(None)), moved + fine_next[...])

    dispatch(
        1, 0, rows,
        lambda d: dot3((wide[0, 0:rows, :], wide[1, 0:rows, :]), (basis[0, :, span(d)], basis[1, :, span(d)])), t, True,
    )

    def columns_use(d, first):
        block = halves(crossed[1, d])

        @pl.loop(0, 2)
        def _(r):
            lines = at(r * half, half)
            term = dot3((basis_t[0, lines, span(d)], basis_t[1, lines, span(d)]), block)
            kept[lines, 0:rows] = term if first else kept[lines, 0:rows] + term

    absorb(1, 1, rows, columns_use, True)

    @pl.loop(0, pieces)
    def _(r):
        block = at(r * piece, piece)
        halves_to(tall, (block, slice(0, rows)), kept[block, 0:rows] * fine_decay(block, span(s)))

    dispatch(2, 0, rows, lambda d: left_rows(d, slice(0, rows)), following, False)
    absorb(2, 1, rows, rows_into(fine_out, 2), False)

    @pl.when((s == low_seat) | (s == low_seat + 1))
    def _():
        for q in range(per_half):
            @pl.when(jnp.logical_not(term_here(q)))
            def _():
                for h in range(cuts):
                    for r in range(pieces):
                        source, target = term_refs(h, r, q)
                        remote(source, target, term_send.at[h, r, q], term_recv.at[h, r], term_place(q)).wait_send()

    @pl.when(jnp.logical_not(to_self))
    def _():
        for slot, source in enumerate((entry, coarse, fine_next, coarse_next)):
            for k in range(2):
                remote(*group_copy(source, slot, k), group_at).wait_send()

    @pl.when(t != last)
    def _():
        pass_guess.wait_send()

    pass_fine.wait_send()
    pass_coarse.wait_send()
    for h in range(cuts):
        swap_terms(h).wait_send()
        swap_states(h).wait_send()
        elsewhere(lambda k: share_out(h, k).wait_send())
        elsewhere(lambda k: fan_out(h, k).wait_send())
    for stage, parts, width, to in ((0, cuts, lanes, t), (1, 1, rows, t), (2, 1, rows, following)):
        @pl.loop(0, count)
        def _(d):
            def leave():
                for h in range(parts):
                    cross(stage, d, h, width, to, s).wait_send()

            if stage == 2:
                leave()
            else:
                pl.when(d != s)(leave)


def on_device(initial, guess, fine, coarse, basis, rates, carried):
    grid, rows = basis.shape[0], initial.shape[0]
    half = grid // 2
    piece, count = half // 2, grid // rows
    per_half, pieces = count // 2, grid // piece
    steps, lanes = 7, 128
    cuts = rows // lanes
    pairs = lax.axis_size("tm") // 2
    share = half // pairs
    f32, bf16 = jnp.float32, jnp.bfloat16
    vmem = pl.BlockSpec(memory_space=pltpu.VMEM)
    dma = pltpu.SemaphoreType.DMA
    fine_new, coarse_new = pl.pallas_call(
        cycle_kernel,
        out_shape=[jax.ShapeDtypeStruct((rows, grid), f32)] * 2,
        in_specs=[vmem] * 6 + [pl.BlockSpec(memory_space=pl.ANY)],
        out_specs=[vmem] * 2,
        scratch_shapes=[
            pltpu.VMEM((2, grid, grid), bf16),
            pltpu.VMEM((2, grid, grid), bf16),
            pltpu.VMEM((grid, lanes), f32),
            pltpu.VMEM((rows, grid), f32),
            pltpu.VMEM((rows, grid), f32),
            pltpu.VMEM((rows, grid), f32),
            pltpu.VMEM((rows, grid), f32),
            pltpu.VMEM((4, half, grid), f32),
            pltpu.VMEM((half, grid), f32),
            pltpu.VMEM((grid, half), f32),
            pltpu.VMEM((grid, half), f32),
            pltpu.VMEM((2, half, grid), bf16),
            pltpu.VMEM((2, grid, half), bf16),
            pltpu.VMEM((2, half, half), bf16),
            pltpu.VMEM((2, half, half), f32),
            pltpu.VMEM((2, half, half), f32),
            pltpu.VMEM((grid, half), f32),
            pltpu.VMEM((grid, rows), f32),
            pltpu.VMEM((half, rows), f32),
            pltpu.VMEM((pairs, share, rows), f32),
            pltpu.VMEM((half, rows), f32),
            pltpu.VMEM((half, rows), f32),
            pltpu.VMEM((3, count, rows, rows), f32),
            pltpu.VMEM((share, rows), f32),
            dma((4, 2)),
            dma((3,)),
            dma((3,)),
            dma((4, count)),
            dma((steps, 2)),
            dma((steps, 2)),
            dma((cuts, pieces, per_half)),
            dma((cuts, pieces)),
            dma((2, cuts)),
            dma((2, cuts)),
            dma((2, cuts, pairs)),
            dma((2, cuts, pairs)),
            dma((3, count, cuts)),
            dma((3, count, cuts)),
            dma((1,)),
        ],
        compiler_params=pltpu.CompilerParams(has_side_effects=True, vmem_limit_bytes=62 * 1024 * 1024),
        cost_estimate=pl.CostEstimate(flops=200_000_000_000, bytes_accessed=16 * grid * grid, transcendentals=0),
        name="cycle",
    )(basis, rates[None, :], guess[0], initial, fine[0], coarse[0], carried)
    return fine_new[None], coarse_new[None]


def solution(mesh):
    placed = (
        P("space", None),
        P("tm", "space", None),
        P("tm", "space", None),
        P("tm", "space", None),
        P(),
        P(),
        P(),
    )
    return jax.shard_map(
        on_device,
        mesh=mesh,
        in_specs=placed,
        out_specs=(P("tm", "space", None), P("tm", "space", None)),
        check_vma=False,
    )
```

time: 291 us -> 241 us (0.83)
  waiting for transfers between devices: 41.9 us -> 0 us
  starting transfers between devices: 10.6 us -> 0 us
  Pallas kernels: 230 us -> 235 us
    ppermute x6 -> x0, waiting for transfers between devices: 41.9 us -> none  [the longest x3 23.7 us: coarse_solve(): arrived[s] = lax.ppermute(sums, 'tm', route)]
    ppermute x6 -> x0, starting transfers between devices: 10.6 us -> none  [the longest x2 7.87 us: swap(): return lax.ppermute(block, 'tm', [(i, i ^ 1) for i in range(count)])]
    pallas_call x2 -> x1, Pallas kernels: 230 us -> 235 us  [on_device(): pl.pallas_call(cycle_kernel, out_shape=[jax.ShapeDtypeStruct((rows, grid)...]
  transfers between devices with their start and end apart: 6 -> 0, of which waited for: 5 -> 0; matrix products, arithmetic and copies ran while one was open for 0% -> 0% of each run, Pallas kernels for 0% -> 0%
where the time goes in v3:
time: 241 us; the launch traced here: 240 us
  Pallas kernels  235 us (98%)
  local copies, waits for them, and re-layouts  4.61 us (2%)
    pallas_call x1, Pallas kernels, on_device(): pl.pallas_call(cycle_kernel, out_shape=[jax.ShapeDtypeStruct((rows, grid)...  235 us

profile of v3, /device:TPU:12, one launch (start us, length us, event | category | flops | bytes accessed | tf_op | source)
XLA Modules:
  0.0 240.0 jit_solution(10897346549280534113)
XLA Ops:
  0.6 234.7 %cycle.1 = (f32[256,1024]{1,0:T(8,128)}, f32[256,1024]{1,0:T(8,128)}) custom-call(f32[1024,1024]{1,0:T(8,128)} %raw.1, f32[1,1024]{1,0:T(1,128)} %bitcast.11, f32[256,1024]{1,0:T(8,128)} %bitcast.8, f32[256,1024]{1,0:T(8,128)} %initial.1, f32[256,1024]{1,0:T(8,128)} %bitcast.9, f32[256,1024]{1,0:T(8,128)} %bitcast.10, f32[1024,1024]{1,0:T(8,128)} %carried.1), custom_call_target="tpu_custom_call" | custom-call | flops 199999995904 | bytes 16777216 | tf_op jit(solution)/shard_map/cycle/pallas_call | solution.py:592
  235.4 2.3 copy.11
  237.7 2.3 copy.12

commit v4 on v3

--- a/solution.py
+++ b/solution.py
@@ -24,16 +24,16 @@
 
 
 def cycle_kernel(
-    raw, rates, guess, initial, fine, coarse, carried, fine_out, coarse_out,
-    basis, basis_t, rates_tall, before, entry, fine_next, coarse_next, slots, field, coeffs, kept, wide, tall, part,
+    raw, guess, initial, fine, coarse, carried, rates, fine_out, coarse_out,
+    basis, basis_t, rates_tall, fine_here, before, entry, fine_next, coarse_next, slots, field, coeffs, kept, wide, tall, part,
     sent, held, decay, landed, joined, gathered, evens, got, crossed, start,
     home_send, shift_send, shift_recv, slot_recv, ex_send, ex_recv, term_send, term_recv,
-    pair_send, pair_recv, share_send, share_recv, cross_send, cross_recv, start_sem,
+    pair_send, pair_recv, share_send, share_recv, cross_send, cross_recv, load_sem,
 ):
     groups, count = lax.axis_size("tm"), lax.axis_size("space")
     t, s = lax.axis_index("tm"), lax.axis_index("space")
     grid = raw.shape[0]
-    rows = fine.shape[0]
+    rows = fine_here.shape[0]
     short = rows // 2
     half = grid // 2
     piece = half // 2
@@ -85,80 +85,116 @@
         def _():
             pltpu.make_async_copy(part_of, dst, recv).start()
 
+    def leave_home(src, slot):
+        @pl.when(jnp.logical_not(to_self))
+        def _():
+            for k in range(2):
+                remote(*group_copy(src, slot, k), group_at).wait_send()
+
     def pass_on(index, src, dst, where):
         return remote(src, dst, shift_send.at[index], shift_recv.at[index], (where, s))
 
-    pass_guess = pass_on(0, guess, before, following)
-    pass_fine = pass_on(1, fine, fine_next, preceding)
-    pass_entry = pass_on(1, entry, fine_next, preceding)
-    pass_coarse = pass_on(2, coarse, coarse_next, preceding)
+    def pass_guess(k):
+        lines = at(k * short, short)
+        return pass_on(k, guess.at[lines], before.at[lines], following)
+
+    pass_fine = pass_on(2, fine, fine_next, preceding)
+    pass_entry = pass_on(2, entry, fine_next, preceding)
+    pass_coarse = pass_on(3, coarse, coarse_next, preceding)
 
     side = t % 2
     pair = t // 2
     own, other = at(side * half, half), at((1 - side) * half, half)
     partner = (core(t, 1 - side), s)
     start_copy = pltpu.make_async_copy(
-        carried.at[at(side * half + pair * share, share), span(s)], start, start_sem.at[0]
+        carried.at[at(side * half + pair * share, share), span(s)], start, load_sem.at[0]
     )
+    load_fine = pltpu.make_async_copy(fine, fine_here, load_sem.at[1])
+    load_initial = pltpu.make_async_copy(initial, before, load_sem.at[2])
+    load_low = pltpu.make_async_copy(raw.at[:, 0:half], coeffs, load_sem.at[3])
+    load_high = pltpu.make_async_copy(raw.at[:, half:grid], kept, load_sem.at[4])
 
     @pl.when(t != last)
     def _():
-        pass_guess.start()
+        pass_guess(0).start()
+        pass_guess(1).start()
+
+    load_fine.start()
+
+    @pl.when(t == 0)
+    def _():
+        load_initial.start()
+
+    load_low.start()
+    load_high.start()
+    start_copy.start()
+
+    @pl.when(t % 2 == 0)
+    def _():
+        to_group(coarse, 1, 0)
+
+    load_fine.wait()
+
+    @pl.when(t == 0)
+    def _():
+        load_initial.wait()
+
+    for k in range(2):
+        @pl.when(t != 0)
+        def _():
+            pass_guess(k).wait_recv()
+
+        lines = at(k * short, short)
+        entry[lines, :] = reacted(before[lines, :]) + fine_here[lines, :]
+        to_group(entry, 0, k)
+
+    @pl.when(t == 0)
+    def _():
+        pass_entry.start()
 
     @pl.when(t != 0)
     def _():
         pass_fine.start()
 
-    @pl.when(t == 0)
-    def _():
-        entry[...] = reacted(initial[...]) + fine[...]
-        pass_entry.start()
-
-    pass_coarse.start()
-    start_copy.start()
-
-    @pl.when(t % 2 == 0)
-    def _():
-        to_group(coarse, 1, 0)
-
-    @pl.when(t != 0)
-    def _():
-        pass_guess.wait_recv()
-        entry[...] = reacted(before[...]) + fine[...]
-
-    to_group(entry, 0, 0)
-    to_group(entry, 0, 1)
-
-    @pl.when(t % 2 == 1)
-    def _():
-        to_group(coarse, 1, 0)
-
-    to_group(coarse, 1, 1)
-
-    @pl.loop(0, count)
-    def _(r):
-        high, low = halves(raw[span(r), :])
-        basis[0, span(r), :] = high
-        basis[1, span(r), :] = low
-
-    pass_fine.wait_recv()
-    to_group(fine_next, 2, 0)
-    to_group(fine_next, 2, 1)
-    pass_coarse.wait_recv()
-    to_group(coarse_next, 3, 0)
-    to_group(coarse_next, 3, 1)
-
-    @pl.loop(0, pieces)
-    def _(r):
+    load_low.wait()
+    load_high.wait()
+    for which, ref in enumerate((coeffs, kept)):
+        @pl.loop(0, count)
+        def _(r):
+            high, low = halves(ref[span(r), :])
+            basis[0, span(r), which * half:(which + 1) * half] = high
+            basis[1, span(r), which * half:(which + 1) * half] = low
+
         @pl.loop(0, pieces)
         def _(c):
-            high, low = halves(raw[at(c * piece, piece), at(r * piece, piece)].T)
-            basis_t[0, at(r * piece, piece), at(c * piece, piece)] = high
-            basis_t[1, at(r * piece, piece), at(c * piece, piece)] = low
+            for r in range(2):
+                lines = slice(which * half + r * piece, which * half + (r + 1) * piece)
+                high, low = halves(ref[at(c * piece, piece), r * piece:(r + 1) * piece].T)
+                basis_t[0, lines, at(c * piece, piece)] = high
+                basis_t[1, lines, at(c * piece, piece)] = low
 
     @pl.loop(0, grid // lanes)
     def _(r):
         rates_tall[at(r * lanes, lanes), :] = jnp.broadcast_to(rates[:, at(r * lanes, lanes)], (lanes, lanes)).T
+
+    leave_home(entry, 0)
+
+    @pl.when(t % 2 == 1)
+    def _():
+        to_group(coarse, 1, 0)
+
+    to_group(coarse, 1, 1)
+    pass_coarse.start()
+
+    def home_fine():
+        pass_fine.wait_recv()
+        to_group(fine_next, 2, 0)
+        to_group(fine_next, 2, 1)
+
+    def home_coarse():
+        pass_coarse.wait_recv()
+        to_group(coarse_next, 3, 0)
+        to_group(coarse_next, 3, 1)
 
     def sums_of_rates(block, columns):
         return rates_tall[block, :1] + rates[:, columns]
@@ -175,7 +211,7 @@
         local = (group == t) & (side * per_half + index == s)
         for k in range(2):
             dst = slots.at[slot, at(index * rows + k * short, short)]
-            src, recv = fine.at[at(k * short, short)], slot_recv.at[slot, 2 * index + k]
+            src, recv = entry.at[at(k * short, short)], slot_recv.at[slot, 2 * index + k]
 
             @pl.when(jnp.logical_not(local))
             def _():
@@ -298,7 +334,24 @@
         def _():
             remote(source, target, term_send.at[h, r, q], term_recv.at[h, r], term_place(q)).start()
 
-    @pl.when((s == low_seat) | (s == low_seat + 1))
+    def leave_terms(h):
+        for q in range(per_half):
+            @pl.when(jnp.logical_not(term_here(q)))
+            def _():
+                for r in range(pieces):
+                    source, target = term_refs(h, r, q)
+                    remote(source, target, term_send.at[h, r, q], term_recv.at[h, r], term_place(q)).wait_send()
+
+    holds = (s == low_seat) | (s == low_seat + 1)
+
+    @pl.when(jnp.logical_not(holds))
+    def _():
+        leave_home(coarse, 1)
+        home_fine()
+        leave_home(fine_next, 2)
+        home_coarse()
+
+    @pl.when(holds)
     def _():
         @pl.loop(0, pieces)
         def _(r):
@@ -322,8 +375,10 @@
 
         forward(0, lambda block: slots[0, block, :], 0, plain)
         inverse(1)
+        home_fine()
         forward(2, from_field(1), 1, keep)
         inverse(3)
+        home_coarse()
         forward(4, from_field(2), 2, plain)
         inverse(5)
 
@@ -344,8 +399,15 @@
                     coeffs[block, at((h * per_half + q) * lanes, lanes)] = (
                         value[:, q * lanes:(q + 1) * lanes] * decay[block, natural] - kept[block, natural]
                     )
-                for q in range(per_half):
-                    send_term(h, r, q)
+                if h == 0:
+                    for q in range(per_half):
+                        send_term(h, r, q)
+
+            if h > 0:
+                leave_terms(h - 1)
+                for r in range(pieces):
+                    for q in range(per_half):
+                        send_term(h, r, q)
 
         for stage in (5, 6):
             for m in range(2):
@@ -537,25 +599,18 @@
     dispatch(2, 0, rows, lambda d: left_rows(d, slice(0, rows)), following, False)
     absorb(2, 1, rows, rows_into(fine_out, 2), False)
 
-    @pl.when((s == low_seat) | (s == low_seat + 1))
-    def _():
-        for q in range(per_half):
-            @pl.when(jnp.logical_not(term_here(q)))
-            def _():
-                for h in range(cuts):
-                    for r in range(pieces):
-                        source, target = term_refs(h, r, q)
-                        remote(source, target, term_send.at[h, r, q], term_recv.at[h, r], term_place(q)).wait_send()
-
-    @pl.when(jnp.logical_not(to_self))
-    def _():
-        for slot, source in enumerate((entry, coarse, fine_next, coarse_next)):
-            for k in range(2):
-                remote(*group_copy(source, slot, k), group_at).wait_send()
+    @pl.when(holds)
+    def _():
+        leave_terms(cuts - 1)
+        leave_home(coarse, 1)
+        leave_home(fine_next, 2)
+
+    leave_home(coarse_next, 3)
 
     @pl.when(t != last)
     def _():
-        pass_guess.wait_send()
+        pass_guess(0).wait_send()
+        pass_guess(1).wait_send()
 
     pass_fine.wait_send()
     pass_coarse.wait_send()
@@ -587,17 +642,18 @@
     pairs = lax.axis_size("tm") // 2
     share = half // pairs
     f32, bf16 = jnp.float32, jnp.bfloat16
-    vmem = pl.BlockSpec(memory_space=pltpu.VMEM)
+    vmem, hbm = pl.BlockSpec(memory_space=pltpu.VMEM), pl.BlockSpec(memory_space=pltpu.HBM)
     dma = pltpu.SemaphoreType.DMA
     fine_new, coarse_new = pl.pallas_call(
         cycle_kernel,
         out_shape=[jax.ShapeDtypeStruct((rows, grid), f32)] * 2,
-        in_specs=[vmem] * 6 + [pl.BlockSpec(memory_space=pl.ANY)],
+        in_specs=[hbm] * 6 + [vmem],
         out_specs=[vmem] * 2,
         scratch_shapes=[
             pltpu.VMEM((2, grid, grid), bf16),
             pltpu.VMEM((2, grid, grid), bf16),
             pltpu.VMEM((grid, lanes), f32),
+            pltpu.VMEM((rows, grid), f32),
             pltpu.VMEM((rows, grid), f32),
             pltpu.VMEM((rows, grid), f32),
             pltpu.VMEM((rows, grid), f32),
@@ -620,8 +676,8 @@
             pltpu.VMEM((3, count, rows, rows), f32),
             pltpu.VMEM((share, rows), f32),
             dma((4, 2)),
-            dma((3,)),
-            dma((3,)),
+            dma((4,)),
+            dma((4,)),
             dma((4, count)),
             dma((steps, 2)),
             dma((steps, 2)),
@@ -633,12 +689,12 @@
             dma((2, cuts, pairs)),
             dma((3, count, cuts)),
             dma((3, count, cuts)),
-            dma((1,)),
+            dma((5,)),
         ],
-        compiler_params=pltpu.CompilerParams(has_side_effects=True, vmem_limit_bytes=62 * 1024 * 1024),
+        compiler_params=pltpu.CompilerParams(has_side_effects=True, vmem_limit_bytes=54 * 1024 * 1024),
         cost_estimate=pl.CostEstimate(flops=200_000_000_000, bytes_accessed=16 * grid * grid, transcendentals=0),
         name="cycle",
-    )(basis, rates[None, :], guess[0], initial, fine[0], coarse[0], carried)
+    )(basis, guess[0], initial, fine[0], coarse[0], carried, rates[None, :])
     return fine_new[None], coarse_new[None]
 
 

time: 241 us -> 224 us (0.929)
  Pallas kernels: 235 us -> 219 us
    pallas_call x1, Pallas kernels: 235 us -> 219 us  [on_device(): pl.pallas_call(cycle_kernel, out_shape=[jax.ShapeDtypeStruct((rows, grid)...]
where the time goes in v4:
time: 224 us
  Pallas kernels  219 us (98%)
  local copies, waits for them, and re-layouts  4.61 us (2%)
    pallas_call x1, Pallas kernels, on_device(): pl.pallas_call(cycle_kernel, out_shape=[jax.ShapeDtypeStruct((rows, grid)...  219 us
    unnamed x2, local copies, waits for them, and re-layouts  4.61 us

profile of v4, /device:TPU:12, one launch (start us, length us, event | category | flops | bytes accessed | tf_op | source)
XLA Modules:
  0.0 224.2 jit_solution(12994347852189316393)
XLA Ops:
  0.6 218.9 %cycle.1 = (f32[256,1024]{1,0:T(8,128)}, f32[256,1024]{1,0:T(8,128)}) custom-call(f32[1024,1024]{1,0:T(8,128)} %raw.1, f32[256,1024]{1,0:T(8,128)} %bitcast.8, f32[256,1024]{1,0:T(8,128)} %initial.1, f32[256,1024]{1,0:T(8,128)} %bitcast.9, f32[256,1024]{1,0:T(8,128)} %bitcast.10, f32[1024,1024]{1,0:T(8,128)} %carried.1, f32[1,1024]{1,0:T(1,128)} %bitcast.11), custom_call_target="tpu_custom_call" | custom-call | flops 199999995904 | bytes 16777216 | tf_op jit(solution)/shard_map/cycle/pallas_call | solution.py:647
  219.6 2.3 %copy.11 = f32[1,256,1024]{2,1,0:T(8,128)} copy(f32[1,256,1024]{2,1,0:T(8,128)} %bitcast.7) | data formatting | bytes 2097152
  221.9 2.3 %copy.12 = f32[1,256,1024]{2,1,0:T(8,128)} copy(f32[1,256,1024]{2,1,0:T(8,128)} %bitcast.6) | data formatting | bytes 2097152

commit v5 on v4

--- a/solution.py
+++ b/solution.py
@@ -148,10 +148,6 @@
         entry[lines, :] = reacted(before[lines, :]) + fine_here[lines, :]
         to_group(entry, 0, k)
 
-    @pl.when(t == 0)
-    def _():
-        pass_entry.start()
-
     @pl.when(t != 0)
     def _():
         pass_fine.start()
@@ -178,6 +174,10 @@
         rates_tall[at(r * lanes, lanes), :] = jnp.broadcast_to(rates[:, at(r * lanes, lanes)], (lanes, lanes)).T
 
     leave_home(entry, 0)
+
+    @pl.when(t == 0)
+    def _():
+        pass_entry.start()
 
     @pl.when(t % 2 == 1)
     def _():
@@ -276,7 +276,7 @@
             coeffs[:, columns] = value
             finish(n, columns, value)
 
-    def inverse(stage):
+    def inverse(stage, midway=None):
         free(stage)
 
         @pl.loop(0, pieces)
@@ -296,6 +296,9 @@
         @pl.loop(0, 2)
         def _(m):
             halves_to(part, (at(m * piece, piece), slice(None)), rows_of(m, side))
+
+        if midway is not None:
+            midway()
 
         @pl.loop(0, 2)
         def _(n):
@@ -374,11 +377,10 @@
             return source
 
         forward(0, lambda block: slots[0, block, :], 0, plain)
+        home_fine()
         inverse(1)
-        home_fine()
         forward(2, from_field(1), 1, keep)
-        inverse(3)
-        home_coarse()
+        inverse(3, home_coarse)
         forward(4, from_field(2), 2, plain)
         inverse(5)
 
@@ -691,7 +693,7 @@
             dma((3, count, cuts)),
             dma((5,)),
         ],
-        compiler_params=pltpu.CompilerParams(has_side_effects=True, vmem_limit_bytes=54 * 1024 * 1024),
+        compiler_params=pltpu.CompilerParams(has_side_effects=True, vmem_limit_bytes=50 * 1024 * 1024),
         cost_estimate=pl.CostEstimate(flops=200_000_000_000, bytes_accessed=16 * grid * grid, transcendentals=0),
         name="cycle",
     )(basis, guess[0], initial, fine[0], coarse[0], carried, rates[None, :])

time: 224 us -> 218 us (0.973)
  Pallas kernels: 219 us -> 214 us
    pallas_call x1, Pallas kernels: 219 us -> 214 us  [on_device(): pl.pallas_call(cycle_kernel, out_shape=[jax.ShapeDtypeStruct((rows, grid)...]
    unnamed x2 -> x6, local copies, waits for them, and re-layouts: 4.61 us -> 3.85 us
where the time goes in v5:
time: 218 us
  Pallas kernels  214 us (98%)
  local copies, waits for them, and re-layouts  3.85 us (2%)
    pallas_call x1, Pallas kernels, on_device(): pl.pallas_call(cycle_kernel, out_shape=[jax.ShapeDtypeStruct((rows, grid)...  214 us

profile of v5, /device:TPU:12, one launch (start us, length us, event | category | flops | bytes accessed | tf_op | source)
XLA Modules:
  0.0 218.1 jit_solution(9215674179653280058)
XLA Ops:
  0.6 0.0 copy-start
  0.6 1.2 copy-done
  1.9 0.0 copy-start.1
  1.9 0.7 copy-done.1
  2.5 213.6 %cycle.1 = (f32[256,1024]{1,0:T(8,128)S(1)}, f32[256,1024]{1,0:T(8,128)S(1)}) custom-call(f32[1024,1024]{1,0:T(8,128)} %raw.1, f32[256,1024]{1,0:T(8,128)S(1)} %bitcast.8, f32[256,1024]{1,0:T(8,128)} %initial.1, f32[256,1024]{1,0:T(8,128)} %bitcast.10, f32[256,1024]{1,0:T(8,128)} %bitcast.11, f32[1024,1024]{1,0:T(8,128)} %carried.1, f32[1,1024]{1,0:T(1,128)S(1)} %bitcast.9), custom_call_target="tpu_custom_call" | custom-call | flops 199999995904 | bytes 16777216 | tf_op jit(solution)/shard_map/cycle/pallas_call | solution.py:649
  216.1 1.0 copy.11
  217.1 1.0 copy.12
Async XLA Ops:
  0.6 1.2 copy-start
  1.9 0.7 copy-start.1

commit v6 on v5

--- a/solution.py
+++ b/solution.py
@@ -510,43 +510,58 @@
     def peer(k):
         return jnp.where(s < count // 2, count - 1 - k, k)
 
-    def cross(stage, d, h, width, to, by):
-        window = pl.ds(pl.multiple_of(d * rows + h * width, width), width)
+    thin = [(0, rows, h * lanes, lanes) for h in range(cuts)]
+    cuts_of = (
+        thin[:-1] + [(u * short, short, (cuts - 1) * lanes, lanes) for u in range(2)],
+        [(0, short, 0, rows)] + [(short, short, h * lanes, lanes) for h in range(cuts)],
+        thin,
+    )
+
+    def staged(stage, i, d):
+        row, tall_by, column, wide_by = cuts_of[stage][i]
+        return stage + 1, slice(row, row + tall_by), pl.ds(pl.multiple_of(d * rows + column, lanes), wide_by)
+
+    def landing(stage, i, by):
+        row, tall_by, column, wide_by = cuts_of[stage][i]
+        return stage, by, slice(row, row + tall_by), slice(column, column + wide_by)
+
+    def cross(stage, i, d, to, by):
         return remote(
-            slots.at[stage + 1, 0:rows, window], crossed.at[stage, by, :, at(h * width, width)],
-            cross_send.at[stage, d, h], cross_recv.at[stage, by, h], (to, d),
+            slots.at[staged(stage, i, d)], crossed.at[landing(stage, i, by)],
+            cross_send.at[stage, d, i], cross_recv.at[stage, by, i], (to, d),
         )
 
-    def dispatch(stage, h, width, block_for, to, keeps):
+    def put(stage, i, d, block, to, keeps=True, later=False):
+        def away():
+            slots[staged(stage, i, d)] = block
+            if not later:
+                cross(stage, i, d, to, s).start()
+
+        if keeps:
+            pl.when(d != s)(away)
+
+            @pl.when(d == s)
+            def _():
+                crossed[landing(stage, i, s)] = block
+        else:
+            away()
+
+    def dispatch(act):
+        @pl.loop(0, count)
+        def _(k):
+            act(peer(k))
+
+    def absorb(stage, waits, use, keeps=True):
+        if keeps:
+            use(s, True)
+
         @pl.loop(0, count)
         def _(k):
             d = peer(k)
-            block = block_for(d)
-
-            def away():
-                slots[stage + 1, 0:rows, pl.ds(pl.multiple_of(d * rows + h * width, width), width)] = block
-                cross(stage, d, h, width, to, s).start()
-
-            if keeps:
-                pl.when(d != s)(away)
-
-                @pl.when(d == s)
-                def _():
-                    crossed[stage, s, :, at(h * width, width)] = block
-            else:
-                away()
-
-    def absorb(stage, parts, width, use, keeps):
-        if keeps:
-            use(s, True)
-
-        @pl.loop(0, count)
-        def _(k):
-            d = peer(k)
 
             def arrive(first):
-                for h in range(parts):
-                    cross(stage, d, h, width, t, d).wait_recv()
+                for i in waits:
+                    cross(stage, i, d, t, d).wait_recv()
                 use(d, first)
 
             if keeps:
@@ -555,51 +570,75 @@
                 pl.when(k == 0)(lambda: arrive(True))
                 pl.when(k != 0)(lambda: arrive(False))
 
-    def left_rows(d, columns):
-        return dot3((basis[0, span(d), :], basis[1, span(d), :]), (tall[0, :, columns], tall[1, :, columns]))
-
-    def rows_into(ref, stage):
+    def left_rows(start_row, size, h):
+        lines, columns = at(start_row, size), slice(h * lanes, (h + 1) * lanes)
+        return dot3((basis[0, lines, :], basis[1, lines, :]), (tall[0, :, columns], tall[1, :, columns]))
+
+    def rows_into(ref, stage, lines):
         def use(d, first):
-            block = halves(crossed[stage, d])
+            block = halves(crossed[stage, d, lines, :])
 
             @pl.loop(0, 2)
             def _(n):
                 columns = at(n * half, half)
                 term = dot3(block, (basis_t[0, span(d), columns], basis_t[1, span(d), columns]))
-                ref[:, columns] = term if first else ref[:, columns] + term
+                ref[lines, columns] = term if first else ref[lines, columns] + term
         return use
 
     for h in range(cuts):
         solve(h)
-        dispatch(0, h, lanes, lambda d: left_rows(d, slice(h * lanes, (h + 1) * lanes)), t, True)
-
-    absorb(0, cuts, lanes, rows_into(coarse_out, 0), True)
-    moved = jnp.where(t == last, 0.0, reacted(coarse_out[...]))
-    halves_to(wide, (slice(0, rows), slice(None)), moved + fine_next[...])
-
-    dispatch(
-        1, 0, rows,
-        lambda d: dot3((wide[0, 0:rows, :], wide[1, 0:rows, :]), (basis[0, :, span(d)], basis[1, :, span(d)])), t, True,
-    )
-
-    def columns_use(d, first):
-        block = halves(crossed[1, d])
-
-        @pl.loop(0, 2)
+        if h < cuts - 1:
+            dispatch(lambda d: put(0, h, d, left_rows(d * rows, rows, h), t))
+        else:
+            for u in range(2):
+                dispatch(lambda d: put(0, h + u, d, left_rows(d * rows + u * short, short, h), t))
+
+    for u in range(2):
+        lines = slice(u * short, (u + 1) * short)
+        absorb(0, range(cuts) if u == 0 else [cuts], rows_into(coarse_out, 0, lines))
+        moved = jnp.where(t == last, 0.0, reacted(coarse_out[lines, :]))
+        halves_to(wide, (lines, slice(None)), moved + fine_next[lines, :])
+
+        def right_part(d):
+            block = dot3((wide[0, lines, :], wide[1, lines, :]), (basis[0, :, span(d)], basis[1, :, span(d)]))
+            if u == 0:
+                put(1, 0, d, block, t)
+            else:
+                for h in range(cuts):
+                    put(1, 1 + h, d, block[:, h * lanes:(h + 1) * lanes], t, later=h > 0)
+
+        dispatch(right_part)
+
+    def send_rest(d):
+        @pl.when(d != s)
+        def _():
+            for h in range(1, cuts):
+                cross(1, 1 + h, d, t, s).start()
+
+    dispatch(send_rest)
+
+    for h in range(cuts):
+        columns = slice(h * lanes, (h + 1) * lanes)
+
+        def columns_use(d, first):
+            block = halves(crossed[1, d, :, columns])
+
+            @pl.loop(0, 2)
+            def _(r):
+                lines = at(r * half, half)
+                term = dot3((basis_t[0, lines, span(d)], basis_t[1, lines, span(d)]), block)
+                kept[lines, columns] = term if first else kept[lines, columns] + term
+
+        absorb(1, [0, 1] if h == 0 else [1 + h], columns_use)
+
+        @pl.loop(0, pieces)
         def _(r):
-            lines = at(r * half, half)
-            term = dot3((basis_t[0, lines, span(d)], basis_t[1, lines, span(d)]), block)
-            kept[lines, 0:rows] = term if first else kept[lines, 0:rows] + term
-
-    absorb(1, 1, rows, columns_use, True)
-
-    @pl.loop(0, pieces)
-    def _(r):
-        block = at(r * piece, piece)
-        halves_to(tall, (block, slice(0, rows)), kept[block, 0:rows] * fine_decay(block, span(s)))
-
-    dispatch(2, 0, rows, lambda d: left_rows(d, slice(0, rows)), following, False)
-    absorb(2, 1, rows, rows_into(fine_out, 2), False)
+            block = at(r * piece, piece)
+            halves_to(tall, (block, columns), kept[block, columns] * fine_decay(block, column_of(h)))
+
+        dispatch(lambda d: put(2, h, d, left_rows(d * rows, rows, h), following, keeps=False))
+
+    absorb(2, range(cuts), rows_into(fine_out, 2, slice(0, rows)), keeps=False)
 
     @pl.when(holds)
     def _():
@@ -621,12 +660,12 @@
         swap_states(h).wait_send()
         elsewhere(lambda k: share_out(h, k).wait_send())
         elsewhere(lambda k: fan_out(h, k).wait_send())
-    for stage, parts, width, to in ((0, cuts, lanes, t), (1, 1, rows, t), (2, 1, rows, following)):
+    for stage, to in ((0, t), (1, t), (2, following)):
         @pl.loop(0, count)
         def _(d):
             def leave():
-                for h in range(parts):
-                    cross(stage, d, h, width, to, s).wait_send()
+                for i in range(len(cuts_of[stage])):
+                    cross(stage, i, d, to, s).wait_send()
 
             if stage == 2:
                 leave()
@@ -689,8 +728,8 @@
             dma((2, cuts)),
             dma((2, cuts, pairs)),
             dma((2, cuts, pairs)),
-            dma((3, count, cuts)),
-            dma((3, count, cuts)),
+            dma((3, count, cuts + 1)),
+            dma((3, count, cuts + 1)),
             dma((5,)),
         ],
         compiler_params=pltpu.CompilerParams(has_side_effects=True, vmem_limit_bytes=50 * 1024 * 1024),

time: 218 us -> 213 us (0.977)
  Pallas kernels: 214 us -> 207 us
    pallas_call x1, Pallas kernels: 214 us -> 207 us  [on_device(): pl.pallas_call(cycle_kernel, out_shape=[jax.ShapeDtypeStruct((rows, grid)...]
where the time goes in v6:
time: 213 us; the launch traced here: 212 us
  Pallas kernels  207 us (97%)
  local copies, waits for them, and re-layouts  3.85 us (2%)
    pallas_call x1, Pallas kernels, on_device(): pl.pallas_call(cycle_kernel, out_shape=[jax.ShapeDtypeStruct((rows, grid)...  207 us

profile of v6, /device:TPU:12, one launch (start us, length us, event | category | flops | bytes accessed | tf_op | source)
XLA Modules:
  0.0 211.9 jit_solution(9366787316794396814)
XLA Ops:
  0.6 0.0 copy-start
  0.6 1.2 copy-done
  1.9 0.0 copy-start.1
  1.9 0.7 copy-done.1
  2.5 207.5 %cycle.1 = (f32[256,1024]{1,0:T(8,128)S(1)}, f32[256,1024]{1,0:T(8,128)S(1)}) custom-call(f32[1024,1024]{1,0:T(8,128)} %raw.1, f32[256,1024]{1,0:T(8,128)S(1)} %bitcast.8, f32[256,1024]{1,0:T(8,128)} %initial.1, f32[256,1024]{1,0:T(8,128)} %bitcast.10, f32[256,1024]{1,0:T(8,128)} %bitcast.11, f32[1024,1024]{1,0:T(8,128)} %carried.1, f32[1,1024]{1,0:T(1,128)S(1)} %bitcast.9), custom_call_target="tpu_custom_call" | custom-call | flops 199999995904 | bytes 16777216 | tf_op jit(solution)/shard_map/cycle/pallas_call | solution.py:688
  210.0 1.0 copy.11
  211.0 1.0 copy.12
Async XLA Ops:
  0.6 1.2 copy-start
  1.9 0.7 copy-start.1

commit v7 on v6

--- a/solution.py
+++ b/solution.py
@@ -26,7 +26,7 @@
 def cycle_kernel(
     raw, guess, initial, fine, coarse, carried, rates, fine_out, coarse_out,
     basis, basis_t, rates_tall, fine_here, before, entry, fine_next, coarse_next, slots, field, coeffs, kept, wide, tall, part,
-    sent, held, decay, landed, joined, gathered, evens, got, crossed, start,
+    sent, held, decay, landed, gathered, evens, got, crossed, start,
     home_send, shift_send, shift_recv, slot_recv, ex_send, ex_recv, term_send, term_recv,
     pair_send, pair_recv, share_send, share_recv, cross_send, cross_recv, load_sem,
 ):
@@ -314,36 +314,37 @@
                 (part[0], part[1]), (basis_t[0, other, columns], basis_t[1, other, columns])
             )
 
-    def term_place(q):
-        return group, side * per_half + q
-
-    def term_refs(h, r, q):
-        block = at(r * piece, piece)
-        source = coeffs.at[block, at((h * per_half + q) * lanes, lanes)]
-        return source, landed.at[block, at(h * lanes, lanes)]
-
-    def term_here(q):
-        where = term_place(q)
+    def term_place(r, q):
+        return core(group, r // 2), side * per_half + q
+
+    def term_refs(h, r, q, parity):
+        source = coeffs.at[at(r * piece, piece), at((h * per_half + q) * lanes, lanes)]
+        target = landed.at[parity, at((r % 2) * piece, piece), at(h * lanes, lanes)]
+        return source, target, term_recv.at[h, 2 * parity + r % 2]
+
+    def term_here(r, q):
+        where = term_place(r, q)
         return (where[0] == t) & (where[1] == s)
 
+    def term_copy(h, r, q):
+        source, target, recv = term_refs(h, r, q, group % 2)
+        return remote(source, target, term_send.at[h, r, q], recv, term_place(r, q))
+
     def send_term(h, r, q):
-        source, target = term_refs(h, r, q)
-
-        @pl.when(term_here(q))
-        def _():
-            pltpu.make_async_copy(source, target, term_recv.at[h, r]).start()
-
-        @pl.when(jnp.logical_not(term_here(q)))
-        def _():
-            remote(source, target, term_send.at[h, r, q], term_recv.at[h, r], term_place(q)).start()
+        @pl.when(term_here(r, q))
+        def _():
+            pltpu.make_async_copy(*term_refs(h, r, q, group % 2)).start()
+
+        @pl.when(jnp.logical_not(term_here(r, q)))
+        def _():
+            term_copy(h, r, q).start()
 
     def leave_terms(h):
-        for q in range(per_half):
-            @pl.when(jnp.logical_not(term_here(q)))
-            def _():
-                for r in range(pieces):
-                    source, target = term_refs(h, r, q)
-                    remote(source, target, term_send.at[h, r, q], term_recv.at[h, r], term_place(q)).wait_send()
+        for r in range(pieces):
+            for q in range(per_half):
+                @pl.when(jnp.logical_not(term_here(r, q)))
+                def _():
+                    term_copy(h, r, q).wait_send()
 
     holds = (s == low_seat) | (s == low_seat + 1)
 
@@ -415,19 +416,18 @@
             for m in range(2):
                 exchange(stage, m).wait_send()
 
-    sender = (core(t, s // per_half), seat(t))
-    from_self = (sender[0] == t) & (sender[1] == s)
-
-    def wait_term(h, r):
-        source, target = term_refs(h, r, 0)
+    def wait_term(h, parity, k):
+        member = core(t, parity)
+        from_self = (core(t, s // per_half) == t) & (seat(member) == s)
+        source, target, recv = term_refs(h, k, 0, parity)
 
         @pl.when(from_self)
         def _():
-            pltpu.make_async_copy(source, target, term_recv.at[h, r]).wait()
+            pltpu.make_async_copy(source, target, recv).wait()
 
         @pl.when(jnp.logical_not(from_self))
         def _():
-            remote(source, target, term_send.at[h, r, 0], term_recv.at[h, r], (t, s)).wait_recv()
+            remote(source, target, term_send.at[h, k, 0], recv, (t, s)).wait_recv()
 
     spread, fanned, given = (slots.at[0, :, at(k * rows, rows)] for k in range(3))
 
@@ -437,11 +437,8 @@
     def column_of(h):
         return at(s * rows + h * lanes, lanes)
 
-    def swap_terms(h):
-        return remote(landed.at[other, cut(h)], joined.at[:, cut(h)], pair_send.at[0, h], pair_recv.at[0, h], partner)
-
     def swap_states(h):
-        return remote(given.at[:, cut(h)], got.at[:, cut(h)], pair_send.at[1, h], pair_recv.at[1, h], partner)
+        return remote(given.at[:, cut(h)], got.at[:, cut(h)], pair_send.at[h], pair_recv.at[h], partner)
 
     def share_out(h, k):
         return remote(
@@ -474,18 +471,18 @@
             def _():
                 act(k)
 
-    def solve(h):
-        for r in range(pieces):
-            wait_term(h, r)
-        swap_terms(h).start()
+    def open_solve(h):
         rate = coarse_decay(own, column_of(h))
-        swap_terms(h).wait_recv()
-        mine, theirs = landed[own, cut(h)], joined[:, cut(h)]
-        first = jnp.where(side == 0, mine, theirs)
-        second = jnp.where(side == 0, theirs, mine)
+        for parity in range(2):
+            for k in range(2):
+                wait_term(h, parity, k)
+        first, second = landed[0, :, cut(h)], landed[1, :, cut(h)]
         spread[:, cut(h)] = second + jnp.where(pair == pairs - 1, 0.0, rate * first)
         elsewhere(lambda k: share_out(h, k).start())
         gathered[pair, :, cut(h)] = spread[at(pair * share, share), cut(h)]
+
+    def close_solve(h):
+        first, rate = landed[0, :, cut(h)], coarse_decay(own, column_of(h))
         if h == 0:
             start_copy.wait()
         elsewhere(lambda k: share_in(h, k).wait_recv())
@@ -585,9 +582,11 @@
                 ref[lines, columns] = term if first else ref[lines, columns] + term
         return use
 
+    open_solve(0)
     for h in range(cuts):
-        solve(h)
+        close_solve(h)
         if h < cuts - 1:
+            open_solve(h + 1)
             dispatch(lambda d: put(0, h, d, left_rows(d * rows, rows, h), t))
         else:
             for u in range(2):
@@ -656,7 +655,6 @@
     pass_fine.wait_send()
     pass_coarse.wait_send()
     for h in range(cuts):
-        swap_terms(h).wait_send()
         swap_states(h).wait_send()
         elsewhere(lambda k: share_out(h, k).wait_send())
         elsewhere(lambda k: fan_out(h, k).wait_send())
@@ -709,8 +707,7 @@
             pltpu.VMEM((2, half, half), f32),
             pltpu.VMEM((2, half, half), f32),
             pltpu.VMEM((grid, half), f32),
-            pltpu.VMEM((grid, rows), f32),
-            pltpu.VMEM((half, rows), f32),
+            pltpu.VMEM((2, half, rows), f32),
             pltpu.VMEM((pairs, share, rows), f32),
             pltpu.VMEM((half, rows), f32),
             pltpu.VMEM((half, rows), f32),
@@ -724,8 +721,8 @@
             dma((steps, 2)),
             dma((cuts, pieces, per_half)),
             dma((cuts, pieces)),
-            dma((2, cuts)),
-            dma((2, cuts)),
+            dma((cuts,)),
+            dma((cuts,)),
             dma((2, cuts, pairs)),
             dma((2, cuts, pairs)),
             dma((3, count, cuts + 1)),

time: 213 us -> 210 us (0.986)
    pallas_call x1, Pallas kernels: 207 us -> 205 us  [on_device(): pl.pallas_call(cycle_kernel, out_shape=[jax.ShapeDtypeStruct((rows, grid)...]
where the time goes in v7:
time: 210 us; the launch traced here: 209 us
  Pallas kernels  205 us (98%)
  local copies, waits for them, and re-layouts  3.85 us (2%)
    pallas_call x1, Pallas kernels, on_device(): pl.pallas_call(cycle_kernel, out_shape=[jax.ShapeDtypeStruct((rows, grid)...  205 us

profile of v7, /device:TPU:12, one launch (start us, length us, event | category | flops | bytes accessed | tf_op | source)
XLA Modules:
  0.0 209.4 jit_solution(8494763307368799283)
XLA Ops:
  0.6 0.0 copy-start
  0.6 1.2 copy-done
  1.9 0.0 copy-start.1
  1.9 0.7 copy-done.1
  2.5 204.9 %cycle.1 = (f32[256,1024]{1,0:T(8,128)S(1)}, f32[256,1024]{1,0:T(8,128)S(1)}) custom-call(f32[1024,1024]{1,0:T(8,128)} %raw.1, f32[256,1024]{1,0:T(8,128)S(1)} %bitcast.8, f32[256,1024]{1,0:T(8,128)} %initial.1, f32[256,1024]{1,0:T(8,128)} %bitcast.10, f32[256,1024]{1,0:T(8,128)} %bitcast.11, f32[1024,1024]{1,0:T(8,128)} %carried.1, f32[1,1024]{1,0:T(1,128)S(1)} %bitcast.9), custom_call_target="tpu_custom_call" | custom-call | flops 199999995904 | bytes 16777216 | tf_op jit(solution)/shard_map/cycle/pallas_call | solution.py:686
  207.4 1.0 copy.11
  208.4 1.0 copy.12
Async XLA Ops:
  0.6 1.2 copy-start
  1.9 0.7 copy-start.1
